TPU v7x, 16 devices: a whole 2x2x2 slice. The times are simulated.
16 devices in a mesh: rep: 1, r: 4 (over y, z), s: 4 (over x, core).
Axes of the slice: x: 2, y: 2, z: 2, core: 2. Of those that a mesh axis runs over, the one named last changes fastest.
Arguments:
- x: bfloat16 [16, 4096, 1024], P(('rep', 'r', 's'))
- dy: bfloat16 [16, 4096, 1024], P(('rep', 'r', 's'))
- w_gate: bfloat16 [2, 1024, 2816], P(None, 's')
- w_up: bfloat16 [2, 1024, 2816], P(None, 's')
- w_down: bfloat16 [2, 2816, 1024], P(None, 's')
- m_w_gate: float32 [2, 1024, 2816], P(None, 's')
- m_w_up: float32 [2, 1024, 2816], P(None, 's')
- m_w_down: float32 [2, 2816, 1024], P(None, 's')
- v_w_gate: float32 [2, 1024, 2816], P(None, 's')
- v_w_up: float32 [2, 1024, 2816], P(None, 's')
- v_w_down: float32 [2, 2816, 1024], P(None, 's')
Outputs:
- output 1: bfloat16 [2, 1024, 2816], P('rep', 's')
- output 2: bfloat16 [2, 1024, 2816], P('rep', 's')
- output 3: bfloat16 [2, 2816, 1024], P('rep', 's')
- output 4: float32 [2, 1024, 2816], P('rep', 's')
- output 5: float32 [2, 1024, 2816], P('rep', 's')
- output 6: float32 [2, 2816, 1024], P('rep', 's')
- output 7: float32 [2, 1024, 2816], P('rep', 's')
- output 8: float32 [2, 1024, 2816], P('rep', 's')
- output 9: float32 [2, 2816, 1024], P('rep', 's')
All inputs are finite; a program needn't handle non-finite values.
Results may differ from a plain program's by a relative error of at most 0.02.
Values are sent between devices in bfloat16 or wider.
A program may use at most 2 GiB of HBM per device.

v0:
```python
import jax
import jax.numpy as jnp
from jax import lax
from jax.sharding import PartitionSpec as P

NAMES = ("w_gate", "w_up", "w_down")


def matmul(a, w):
    return jnp.dot(a, w, preferred_element_type=jnp.float32).astype(jnp.bfloat16)


def normed(h):
    wide = h.astype(jnp.float32)
    scale = lax.rsqrt(jnp.mean(wide**2, -1, keepdims=True) + 1e-6)
    return (wide * scale).astype(jnp.bfloat16)


def layer(h, w):
    a = normed(h)
    gate = jnp.dot(a, w["w_gate"], preferred_element_type=jnp.float32)
    up = jnp.dot(a, w["w_up"], preferred_element_type=jnp.float32)
    return h + matmul((jax.nn.silu(gate) * up).astype(jnp.bfloat16), w["w_down"])


def adamw(w, m, v, g):
    m = 0.9 * m + 0.1 * g
    v = 0.95 * v + 0.05 * g * g
    step = m * lax.rsqrt(v + 1e-8) + 0.1 * w
    return (w - 0.02 * step).astype(jnp.bfloat16), m, v


def solution(mesh):
    def fetched(weights, number):
        return {name: lax.all_gather(w[number], "s", axis=0, tiled=True) for name, w in zip(NAMES, weights, strict=True)}

    def summed(term):
        return lax.psum(lax.psum_scatter(term, "s", scatter_dimension=0, tiled=True), "r")

    def step(x, dy, *arrays):
        weights, m, v = (arrays[i : i + 3] for i in (0, 3, 6))
        layers = weights[0].shape[0]
        h, kept = x[0], []
        for number in range(layers):
            kept.append(h)
            h = layer(h, fetched(weights, number))
        by_h, mine = dy[0], [None] * layers
        for number in reversed(range(layers)):
            _, back = jax.vjp(lambda w, h: layer(h, w), fetched(weights, number), kept[number])
            by_w, by_h = back(by_h)
            mine[number] = [summed(by_w[name]) for name in NAMES]
        gradients = [jnp.stack([mine[number][i] for number in range(layers)]).astype(jnp.float32) for i in range(3)]
        new = [adamw(w.astype(jnp.float32), m, v, g) for w, m, v, g in zip(weights, m, v, gradients, strict=True)]
        return tuple(one[which] for which in range(3) for one in new)

    states, cut = P(("rep", "r", "s"), None, None), P(None, "s", None)
    return jax.shard_map(
        step,
        mesh=mesh,
        in_specs=(states, states) + (cut,) * 9,
        out_specs=(P("rep", "s", None),) * 9,
        check_vma=False,
    )
```

profile of v0, /device:TPU:0, one launch (start us, length us, event | category | flops | bytes accessed | tf_op | source)
XLA Modules:
  0.0 981.7 jit_solution(15286701341398505508)
XLA Ops:
  7.2 0.0 all-gather.13.cloned.1.call-start
  7.2 3.7 fusion.85
  10.9 0.0 all-gather.13.cloned.1.call-update
  11.0 0.0 all-gather.15.cloned.1.call-start
  11.0 1.8 fusion.84
  12.8 0.0 all-gather.15.cloned.1.call-update
  12.8 0.0 all-gather.17.cloned.1.call-start
  12.9 3.6 fusion.83
  16.5 0.0 all-gather.17.cloned.1.call-update
  16.5 0.0 all-gather.21.cloned.1.call-start
  16.6 0.5 all-gather.21.cloned.1.call-update
  17.1 0.0 all-gather.23.cloned.1.call-start
  17.2 0.5 all-gather.23.cloned.1.call-update
  17.7 0.0 all-gather.19.cloned.1.call-start
  17.7 0.5 all-gather.19.cloned.1.call-update
  18.3 0.0 reduce-scatter.15.cloned.1.call-start
  18.3 12.0 %copy.20 = bf16[1,4096,1024]{1,2,0:T(8,128)(2,1)} copy(bf16[1,4096,1024]{2,1,0:T(8,128)(2,1)} %param.11) | data formatting | bytes 16777216 | tf_op args[0]
  30.3 5.1 fusion.15
  35.4 11.3 %copy.21 = bf16[1,4096,1024]{1,2,0:T(8,128)(2,1)} copy(bf16[1,4096,1024]{2,1,0:T(8,128)(2,1)} %param.12) | data formatting | bytes 16777216 | tf_op args[1]
  46.8 8.7 all-gather.13.cloned.1.call-done
  55.4 32.4 %fusion.53 = f32[4096,2816]{1,0:T(8,128)} fusion(bf16[1,1024,2816]{2,1,0:T(8,128)(2,1)} %all-gather.13.cloned.1.call-done, bf16[1,4096,1024]{1,2,0:T(8,128)(2,1)} %copy.20, f32[4096]{0:T(1024)S(1)} %add_rsqrt_fusion), kind=kOutput, calls=%fused_computation.84 | convolution fusion | flops 23634903040 | bytes 60309504 | tf_op jit(solution)/shard_map/dot_general | solution.py:21
  87.8 11.3 %all-gather.15.cloned.1.call-done = bf16[1,1024,2816]{2,1,0:T(8,128)(2,1)} async-done(((bf16[1,256,2816]{2,1,0:T(8,128)(2,1)}), bf16[1,1024,2816]{2,1,0:T(8,128)(2,1)}) %all-gather.15.cloned.1.call-update) | async-done | bytes 5767184 | tf_op jit(solution)/shard_map/all_gather | solution.py:35
  99.1 54.9 %multiply_convert_fusion.1 = (bf16[4096,2816]{1,0:T(8,128)(2,1)}, f32[4096,2816]{1,0:T(8,128)}) fusion(f32[4096,2816]{1,0:T(8,128)} %fusion.53, bf16[1,1024,2816]{2,1,0:T(8,128)(2,1)} %all-gather.15.cloned.1.call-done, bf16[1,4096,1024]{1,2,0:T(8,128)(2,1)} %copy.20, f32[4096]{0:T(1024)S(1)} %add_rsqrt_fusion), kind=kOutput, calls=%fused_computation.17 | convolution fusion | flops 23704109056 | bytes 129515520 | tf_op jit(solution)/shard_map/dot_general | solution.py:22
  154.0 32.7 %fusion.19 = (f32[4096]{0:T(1024)S(1)}, bf16[4096,1024]{0,1:T(8,128)(2,1)}) fusion(bf16[4096,2816]{1,0:T(8,128)(2,1)} %get-tuple-element.30, bf16[1,2816,1024]{2,1,0:T(8,128)(2,1)} %all-gather.17.cloned.1.call-done, bf16[1,4096,1024]{1,2,0:T(8,128)(2,1)} %copy.20), kind=kOutput, calls=%fused_computation.37 | convolution fusion | flops 23643287552 | bytes 45629440 | tf_op jit(solution)/shard_map/dot_general | solution.py:10
  186.7 0.0 all-gather.21.cloned.1.call-done
  186.8 31.7 %convolution_convert_fusion.1 = bf16[4096,2816]{1,0:T(8,128)(2,1)} fusion(bf16[1,4096,1024]{2,1,0:T(8,128)(2,1)} %param.12, bf16[1,2816,1024]{2,1,0:T(8,128)(2,1)} %all-gather.21.cloned.1.call-done), kind=kOutput, calls=%fused_computation.29 | convolution fusion | flops 23633854464 | bytes 37224448 | tf_op jit(solution)/shard_map/transpose(jvp())/dot_general | solution.py:10
  218.5 11.2 %all-gather.23.cloned.1.call-done = bf16[1,1024,2816]{2,1,0:T(8,128)(2,1)} async-done(((bf16[1,256,2816]{2,1,0:T(8,128)(2,1)}), bf16[1,1024,2816]{2,1,0:T(8,128)(2,1)}) %all-gather.23.cloned.1.call-update) | async-done | bytes 5767184 | tf_op jit(solution)/shard_map/all_gather | solution.py:35
  229.7 32.6 %fusion.41 = f32[4096,2816]{1,0:T(8,128)} fusion(bf16[1,1024,2816]{2,1,0:T(8,128)(2,1)} %all-gather.23.cloned.1.call-done, bf16[4096,1024]{0,1:T(8,128)(2,1)} %get-tuple-element.33, f32[4096]{0:T(1024)S(1)} %fusion.71), kind=kOutput, calls=%fused_computation.72 | convolution fusion | flops 23634903040 | bytes 60309504 | tf_op jit(solution)/shard_map/jvp()/dot_general | solution.py:22
  262.3 10.9 %all-gather.19.cloned.1.call-done = bf16[1,1024,2816]{2,1,0:T(8,128)(2,1)} async-done(((bf16[1,256,2816]{2,1,0:T(8,128)(2,1)}), bf16[1,1024,2816]{2,1,0:T(8,128)(2,1)}) %all-gather.19.cloned.1.call-update) | async-done | bytes 5767184 | tf_op jit(solution)/shard_map/all_gather | solution.py:35
  273.2 62.4 %fusion.2 = (bf16[4096,2816]{1,0:T(8,128)(2,1)}, f32[4096,2816]{1,0:T(8,128)}) fusion(f32[4096,2816]{1,0:T(8,128)} %fusion.41, bf16[4096,2816]{1,0:T(8,128)(2,1)} %convolution_convert_fusion.1, bf16[1,1024,2816]{2,1,0:T(8,128)(2,1)} %all-gather.19.cloned.1.call-done, bf16[4096,1024]{0,1:T(8,128)(2,1)} %get-tuple-element.33, f32[4096]{0:T(1024)S(1)} %fusion.71), kind=kOutput, calls=%fused_computation.8 | convolution fusion | flops 23773315072 | bytes 152584192 | tf_op jit(solution)/shard_map/jvp()/dot_general | solution.py:21
  335.6 28.8 %fusion.45 = bf16[4096,1024]{0,1:T(8,128)(2,1)} fusion(bf16[4096,2816]{1,0:T(8,128)(2,1)} %get-tuple-element.34, bf16[1,1024,2816]{2,1,0:T(8,128)(2,1)S(1)} %copy-done.14), kind=kOutput, calls=%fused_computation.76 | convolution fusion | flops 23622320128 | bytes 37224448 | tf_op jit(solution)/shard_map/transpose(jvp())/dot_general | solution.py:21
  364.4 42.3 %fusion.21 = (f32[4096]{0:T(1024)S(1)}, bf16[4096,1024]{0,1:T(8,128)(2,1)}) fusion(bf16[4096,1024]{0,1:T(8,128)(2,1)} %get-tuple-element.33, bf16[4096,1024]{0,1:T(8,128)(2,1)} %fusion.45, bf16[1,1024,2816]{2,1,0:T(8,128)(2,1)} %all-gather.23.cloned.1.call-done, bf16[4096,2816]{1,0:T(8,128)(2,1)} %convolution_convert_fusion.1, ...), kind=kOutput, calls=%fused_computation.39 | convolution fusion | flops 23716687872 | bytes 100155392 | tf_op jit(solution)/shard_map/transpose(jvp())/dot_general | solution.py:22
  406.7 13.8 %fusion.22 = bf16[4096,1024]{0,1:T(8,128)(2,1)} fusion(bf16[4096,1024]{0,1:T(8,128)(2,1)} %get-tuple-element.33, bf16[4096,1024]{0,1:T(8,128)(2,1)} %get-tuple-element.37, bf16[1,4096,1024]{1,2,0:T(8,128)(2,1)} %copy.21, f32[4096]{0:T(1024)S(1)} %multiply_multiply_fusion.3, f32[4096]{0:T(1024)S(1)} %fusion.71), kind=kLoop, calls=%fused_computation.43 | loop fusion | flops 29360128 | bytes 33587200 | tf_op jit(solution)/shard_map/transpose(jvp())/add_any | solution.py:14
  420.5 33.2 %convolution_convert_fusion.2 = bf16[2816,1024]{1,0:T(8,128)(2,1)} fusion(bf16[4096,2816]{1,0:T(8,128)(2,1)} %get-tuple-element.30, bf16[4096,1024]{0,1:T(8,128)(2,1)} %fusion.22), kind=kOutput, calls=%fused_computation.90 | convolution fusion | flops 23625203712 | bytes 37224448 | tf_op jit(solution)/shard_map/transpose(jvp())/dot_general | solution.py:10
  453.7 0.0 reduce-scatter.15.cloned.1.call-update
  453.7 0.0 reduce-scatter.17.cloned.1.call-start
  453.8 41.1 %fusion.55 = bf16[2816,1024]{1,0:T(8,128)(2,1)} fusion(bf16[1,4096,1024]{2,1,0:T(8,128)(2,1)} %param.12, f32[4096,2816]{1,0:T(8,128)} %fusion.41, f32[4096,2816]{1,0:T(8,128)} %get-tuple-element.35), kind=kOutput, calls=%fused_computation.86 | convolution fusion | flops 23694409728 | bytes 106430464 | tf_op jit(solution)/shard_map/transpose(jvp())/dot_general | solution.py:10
  494.8 0.0 reduce-scatter.17.cloned.1.call-update
  494.9 0.0 reduce-scatter.11.cloned.1.call-start
  494.9 30.7 %convolution_convert_fusion = bf16[4096,2816]{1,0:T(8,128)(2,1)} fusion(bf16[4096,1024]{0,1:T(8,128)(2,1)} %fusion.22, bf16[1,2816,1024]{2,1,0:T(8,128)(2,1)} %all-gather.17.cloned.1.call-done), kind=kOutput, calls=%fused_computation.28 | convolution fusion | flops 23633854464 | bytes 37224448 | tf_op jit(solution)/shard_map/transpose(jvp())/dot_general | solution.py:10
  525.6 36.4 %fusion.62 = bf16[1024,2816]{1,0:T(8,128)(2,1)} fusion(bf16[4096,2816]{1,0:T(8,128)(2,1)} %convolution_convert_fusion, f32[4096,2816]{1,0:T(8,128)} %fusion.53, bf16[1,4096,1024]{1,2,0:T(8,128)(2,1)} %copy.20, f32[4096]{0:T(1024)S(1)} %copy-done.13), kind=kOutput, calls=%fused_computation.89 | convolution fusion | flops 23706992640 | bytes 83378176 | tf_op jit(solution)/shard_map/transpose(jvp())/dot_general | solution.py:22
  562.0 0.0 reduce-scatter.11.cloned.1.call-update
  562.0 0.0 reduce-scatter.13.cloned.1.call-start
  562.1 36.6 %fusion.58 = bf16[1024,2816]{1,0:T(8,128)(2,1)} fusion(bf16[4096,2816]{1,0:T(8,128)(2,1)} %convolution_convert_fusion.1, bf16[4096,1024]{0,1:T(8,128)(2,1)} %get-tuple-element.33, f32[4096]{0:T(1024)S(1)} %copy-done.9, f32[4096,2816]{1,0:T(8,128)} %get-tuple-element.35), kind=kOutput, calls=%fused_computation.87 | convolution fusion | flops 23706992640 | bytes 83378176 | tf_op jit(solution)/shard_map/transpose(jvp())/dot_general | solution.py:22
  598.7 0.0 reduce-scatter.13.cloned.1.call-update
  598.8 0.0 reduce-scatter.7.cloned.1.call-start
  598.8 44.1 %fusion.59 = bf16[1024,2816]{1,0:T(8,128)(2,1)} fusion(f32[4096,2816]{1,0:T(8,128)} %fusion.53, f32[4096,2816]{1,0:T(8,128)} %get-tuple-element.31, bf16[4096,2816]{1,0:T(8,128)(2,1)} %convolution_convert_fusion, bf16[1,4096,1024]{1,2,0:T(8,128)(2,1)} %copy.20, f32[4096]{0:T(1024)S(1)} %copy-done.13), kind=kOutput, calls=%fused_computation.88 | convolution fusion | flops 23764664320 | bytes 129515520 | tf_op jit(solution)/shard_map/transpose(jvp())/dot_general | solution.py:21
  642.9 0.0 reduce-scatter.7.cloned.1.call-update
  642.9 0.0 reduce-scatter.9.cloned.1.call-start
  643.0 33.1 %convolution_convert_fusion.3 = bf16[1024,2816]{1,0:T(8,128)(2,1)} fusion(bf16[4096,2816]{1,0:T(8,128)(2,1)} %get-tuple-element.34, bf16[4096,1024]{0,1:T(8,128)(2,1)} %get-tuple-element.33, f32[4096]{0:T(1024)S(1)} %copy-done.9), kind=kOutput, calls=%fused_computation.91 | convolution fusion | flops 23634903040 | bytes 37240832 | tf_op jit(solution)/shard_map/transpose(jvp())/dot_general | solution.py:21
  676.1 0.0 reduce-scatter.9.cloned.1.call-update
  676.2 0.0 all-reduce.3.cloned.1.call-start
  676.2 0.0 reduce-scatter.15.cloned.1.call-done
  676.2 0.0 reduce-scatter.17.cloned.1.call-done
  676.3 0.0 reduce-scatter.11.cloned.1.call-done
  676.3 0.0 reduce-scatter.13.cloned.1.call-done
  676.3 41.6 %reduce-scatter.7.cloned.1.call-done = bf16[256,2816]{1,0:T(8,128)(2,1)} async-done(((bf16[1024,2816]{1,0:T(8,128)(2,1)}), bf16[256,2816]{1,0:T(8,128)(2,1)}) %reduce-scatter.7.cloned.1.call-update) | async-done | bytes 1441808 | tf_op jit(solution)/shard_map/reduce_scatter | solution.py:38
  717.9 52.9 %reduce-scatter.9.cloned.1.call-done = bf16[256,2816]{1,0:T(8,128)(2,1)} async-done(((bf16[1024,2816]{1,0:T(8,128)(2,1)}), bf16[256,2816]{1,0:T(8,128)(2,1)}) %reduce-scatter.9.cloned.1.call-update) | async-done | bytes 1441808 | tf_op jit(solution)/shard_map/reduce_scatter | solution.py:38
  770.8 0.0 all-reduce.3.cloned.1.call-update
  770.8 172.5 %all-reduce.3.cloned.1.call-done = (bf16[1,256,2816]{2,1,0:T(8,128)(2,1)}, bf16[1,256,2816]{2,1,0:T(8,128)(2,1)}, bf16[1,256,2816]{2,1,0:T(8,128)(2,1)}, bf16[1,...) async-done(((bf16[1,256,2816]{2,1,0:T(8,128)(2,1)}, bf16[1,256,2816]{2,1,0:T(8,128)(2,1)}, bf16[1,256,2816]{2,1,0:T(8,128)(2,1)}, ...) | async-done | bytes 8650768 | tf_op jit(solution)/shard_map/psum | solution.py:38
  943.4 12.0 %fusion.36 = (bf16[2,704,1024]{2,1,0:T(8,128)(2,1)}, f32[2,704,1024]{2,1,0:T(8,128)}, f32[2,704,1024]{2,1,0:T(8,128)}) fusion(bf16[2,704,1024]{2,1,0:T(8,128)(2,1)S(1)} %copy-done.3, bf16[1,704,1024]{2,1,0:T(8,128)(2,1)} %get-tuple-element.13, bf16[1,704,1024]{2,1,0:T(8,128)(2,1)} %get-tuple-element.14, f32[2,704,1024]{2,1,0:T(8,128)} %param.21, ...), kind=kLoop, calls=%fused_computation.67 | loop fusion | flops 27394048 | bytes 31719424 | tf_op jit(solution)/shard_map/convert_element_type | solution.py:30
  955.4 1.0 copy-done.6
  956.4 0.4 copy-done.7
  956.8 18.0 %fusion.28 = (bf16[2,256,2816]{2,1,0:T(8,128)(2,1)}, f32[2,256,2816]{2,1,0:T(8,128)}, f32[2,256,2816]{2,1,0:T(8,128)}, bf16[2,256,2816]{2,1,0:T(8,128)(2,1)}, f3...) fusion(bf16[2,256,2816]{2,1,0:T(8,128)(2,1)S(1)} %copy-done, bf16[1,256,2816]{2,1,0:T(8,128)(2,1)S(1)} %copy-done.4, ...), kind=kLoop, calls=%fused_computation.59 | loop fusion | flops 54788096 | bytes 63438848 | tf_op jit(solution)/shard_map/convert_element_type | solution.py:30
  (32 shorter events, 0.1 us)
Async XLA Ops:
  7.2 3.8 copy-start.1
  7.2 48.3 %all-gather.13.cloned.1.call-start = ((), (), s32[]{:S(2)}) async-start(), calls=%async_computation.12 | async-start | bytes 7208960 | tf_op jit(solution)/shard_map/all_gather | solution.py:35
  11.0 88.1 %all-gather.15.cloned.1.call-start = ((), (), s32[]{:S(2)}) async-start(), calls=%async_computation.13 | async-start | bytes 7208960 | tf_op jit(solution)/shard_map/all_gather | solution.py:35
  12.8 141.2 %all-gather.17.cloned.1.call-start = ((), (), s32[]{:S(2)}) async-start(), calls=%async_computation.14 | async-start | bytes 7208960 | tf_op jit(solution)/shard_map/all_gather | solution.py:35
  16.5 170.2 %all-gather.21.cloned.1.call-start = ((), (), s32[]{:S(2)}) async-start(), calls=%async_computation.16 | async-start | bytes 7208960 | tf_op jit(solution)/shard_map/all_gather | solution.py:35
  17.1 212.6 %all-gather.23.cloned.1.call-start = ((), (), s32[]{:S(2)}) async-start(), calls=%async_computation.17 | async-start | bytes 7208960 | tf_op jit(solution)/shard_map/all_gather | solution.py:35
  17.7 255.5 %all-gather.19.cloned.1.call-start = ((), (), s32[]{:S(2)}) async-start(), calls=%async_computation.15 | async-start | bytes 7208960 | tf_op jit(solution)/shard_map/all_gather | solution.py:35
  18.3 657.9 %reduce-scatter.15.cloned.1.call-start = ((), (), s32[]{:S(2)}) async-start(), calls=%async_computation.10 | async-start | bytes 7208960 | tf_op jit(solution)/shard_map/reduce_scatter | solution.py:38
  35.4 63.7 %copy-start.12 = (f32[4096]{0:T(1024)}, f32[4096]{0:T(1024)S(1)}, u32[]{:S(2)}) copy-start(f32[4096]{0:T(1024)S(1)} %add_rsqrt_fusion) | copy-start | bytes 49156
  186.7 31.8 %copy-start.10 = (f32[4096]{0:T(1024)}, f32[4096]{0:T(1024)S(1)}, u32[]{:S(2)}) copy-start(f32[4096]{0:T(1024)S(1)} %get-tuple-element.32) | copy-start | bytes 49156
  186.7 220.0 %copy-start.8 = (f32[4096]{0:T(1024)}, f32[4096]{0:T(1024)S(1)}, u32[]{:S(2)}) copy-start(f32[4096]{0:T(1024)S(1)} %fusion.71) | copy-start | bytes 49156
  273.2 62.4 %copy-start.14 = (bf16[1,1024,2816]{2,1,0:T(8,128)(2,1)S(1)}, bf16[1,1024,2816]{2,1,0:T(8,128)(2,1)}, u32[]{:S(2)}) copy-start(bf16[1,1024,2816]{2,1,0:T(8,128)(2,1)} %all-gather.19.cloned.1.call-done) | copy-start | bytes 17301508
  364.4 42.3 %copy-start.11 = (f32[4096]{0:T(1024)S(1)}, f32[4096]{0:T(1024)}, u32[]{:S(2)}) copy-start(f32[4096]{0:T(1024)} %copy-done.10) | copy-start | bytes 49156
  453.7 222.5 %reduce-scatter.17.cloned.1.call-start = ((), (), s32[]{:S(2)}) async-start(), calls=%async_computation.11 | async-start | bytes 7208960 | tf_op jit(solution)/shard_map/reduce_scatter | solution.py:38
  494.8 30.8 %copy-start.13 = (f32[4096]{0:T(1024)S(1)}, f32[4096]{0:T(1024)}, u32[]{:S(2)}) copy-start(f32[4096]{0:T(1024)} %copy-done.12) | copy-start | bytes 49156
  494.9 181.4 %reduce-scatter.11.cloned.1.call-start = ((), (), s32[]{:S(2)}) async-start(), calls=%async_computation.8 | async-start | bytes 7208960 | tf_op jit(solution)/shard_map/reduce_scatter | solution.py:38
  525.6 36.5 %copy-start.9 = (f32[4096]{0:T(1024)S(1)}, f32[4096]{0:T(1024)}, u32[]{:S(2)}) copy-start(f32[4096]{0:T(1024)} %copy-done.8) | copy-start | bytes 49156
  562.0 114.3 %reduce-scatter.13.cloned.1.call-start = ((), (), s32[]{:S(2)}) async-start(), calls=%async_computation.9 | async-start | bytes 7208960 | tf_op jit(solution)/shard_map/reduce_scatter | solution.py:38
  598.8 119.2 %reduce-scatter.7.cloned.1.call-start = ((), (), s32[]{:S(2)}) async-start(), calls=%async_computation.6 | async-start | bytes 7208960 | tf_op jit(solution)/shard_map/reduce_scatter | solution.py:38
  642.9 127.8 %reduce-scatter.9.cloned.1.call-start = ((), (), s32[]{:S(2)}) async-start(), calls=%async_computation.7 | async-start | bytes 7208960 | tf_op jit(solution)/shard_map/reduce_scatter | solution.py:38
  676.1 267.2 %copy-start.3 = (bf16[2,704,1024]{2,1,0:T(8,128)(2,1)S(1)}, bf16[2,704,1024]{2,1,0:T(8,128)(2,1)}, u32[]{:S(2)}) copy-start(bf16[2,704,1024]{2,1,0:T(8,128)(2,1)} %param.15) | copy-start | bytes 8650756
  676.2 267.2 %all-reduce.3.cloned.1.call-start = ((), (), s32[]{:S(2)}) async-start(), calls=%async_computation.18 | async-start | bytes 17301504 | tf_op jit(solution)/shard_map/psum | solution.py:38
  943.3 12.0 %copy-start = (bf16[2,256,2816]{2,1,0:T(8,128)(2,1)S(1)}, bf16[2,256,2816]{2,1,0:T(8,128)(2,1)}, u32[]{:S(2)}) copy-start(bf16[2,256,2816]{2,1,0:T(8,128)(2,1)} %param.13) | copy-start | bytes 8650756
  943.3 12.0 %copy-start.2 = (bf16[2,256,2816]{2,1,0:T(8,128)(2,1)S(1)}, bf16[2,256,2816]{2,1,0:T(8,128)(2,1)}, u32[]{:S(2)}) copy-start(bf16[2,256,2816]{2,1,0:T(8,128)(2,1)} %param.14) | copy-start | bytes 8650756
  943.3 12.0 %copy-start.4 = (bf16[1,256,2816]{2,1,0:T(8,128)(2,1)S(1)}, bf16[1,256,2816]{2,1,0:T(8,128)(2,1)}, u32[]{:S(2)}) copy-start(bf16[1,256,2816]{2,1,0:T(8,128)(2,1)} %get-tuple-element.9) | copy-start | bytes 4325380
  943.3 12.0 %copy-start.5 = (bf16[1,256,2816]{2,1,0:T(8,128)(2,1)S(1)}, bf16[1,256,2816]{2,1,0:T(8,128)(2,1)}, u32[]{:S(2)}) copy-start(bf16[1,256,2816]{2,1,0:T(8,128)(2,1)} %get-tuple-element.10) | copy-start | bytes 4325380
  943.4 13.0 %copy-start.6 = (bf16[1,256,2816]{2,1,0:T(8,128)(2,1)S(1)}, bf16[1,256,2816]{2,1,0:T(8,128)(2,1)}, u32[]{:S(2)}) copy-start(bf16[1,256,2816]{2,1,0:T(8,128)(2,1)} %get-tuple-element.11) | copy-start | bytes 4325380
  943.4 13.4 %copy-start.7 = (bf16[1,256,2816]{2,1,0:T(8,128)(2,1)S(1)}, bf16[1,256,2816]{2,1,0:T(8,128)(2,1)}, u32[]{:S(2)}) copy-start(bf16[1,256,2816]{2,1,0:T(8,128)(2,1)} %get-tuple-element.12) | copy-start | bytes 4325380
Sparse Core Ops, SparseCore 0:
  11.1 44.3 all-gather.12
  57.6 41.4 all-gather.14
  101.2 41.4 all-gather.16
  144.7 41.4 all-gather.20
  188.2 41.4 all-gather.22
  231.7 41.4 all-gather.18
  453.8 49.8 reduce-scatter.14
  506.8 49.8 reduce-scatter.16
  562.2 49.8 reduce-scatter.10
  615.0 49.8 reduce-scatter.12
  668.0 49.8 reduce-scatter.6
  720.9 49.8 reduce-scatter.8
  775.5 167.7 all-reduce.2
where the time goes:
time: 989 us; the launch traced here: 982 us
  matrix products  573 us (58%)
  waiting for transfers between devices  311 us (31%)
  other arithmetic  48.8 us (5%)
  local copies, waits for them, and re-layouts  33.9 us (3%)
  between operations  14.5 us (1%)
    dot_general x5, matrix products, layer(): up = jnp.dot(a, w['w_up'], preferred_element_type=jnp.float32)  203 us
    dot_general x5, matrix products, layer(): gate = jnp.dot(a, w['w_gate'], preferred_element_type=jnp.float32)  201 us
    psum x1, waiting for transfers between devices, summed(): lax.psum(lax.psum_scatter(term, 's', scatter_dimension=0, tiled=True), 'r')  173 us
    dot_general x5, matrix products, matmul(): jnp.dot(a, w, preferred_element_type=jnp.float32).astype(jnp.bfloat16)  169 us
    reduce_scatter x6, waiting for transfers between devices, summed(): lax.psum_scatter(term, 's', scatter_dimension=0, tiled=True)  94.5 us
    all_gather x6, waiting for transfers between devices, fetched(): lax.all_gather(w[number], 's', axis=0, tiled=True)  42.1 us
    convert_element_type x2, other arithmetic, adamw(): return ((w - 0.02 * step).astype(jnp.bfloat16), m, v)  30 us
    unnamed x32, local copies, waits for them, and re-layouts  24.8 us
  transfers between devices with their start and end apart: 13, of which 7 were waited for; matrix products, arithmetic and copies ran while one was open for 45% of the time, Pallas kernels for 0%

commit v1 on v0

v1 whole, which is shorter than its diff:
```python
import functools

import jax
import jax.numpy as jnp
from jax import lax
from jax.experimental import pallas as pl
from jax.experimental.pallas import tpu as pltpu
from jax.sharding import PartitionSpec as P

NAMES = ("w_gate", "w_up", "w_down")
BF, F32 = jnp.bfloat16, jnp.float32
MESH = pl.DeviceIdType.MESH
NN, TB, TA = ((((1,), (0,)), ((), ())), (((1,), (1,)), ((), ())), (((0,), (0,)), ((), ())))
VMEM = 60 * 2**20


def dot(a, b, dims):
    return lax.dot_general(a, b, dims, preferred_element_type=F32)


def whole(w):
    return jnp.concatenate([w[s] for s in range(4)], axis=1)


def scale_of(wide):
    return lax.rsqrt(jnp.mean(wide * wide, -1, keepdims=True) + 1e-6)


def normed(h):
    wide = h.astype(F32)
    return (wide * scale_of(wide)).astype(BF)


def adamw(w, m, v, g):
    m = 0.9 * m + 0.1 * g
    v = 0.95 * v + 0.05 * g * g
    step = m * lax.rsqrt(v + 1e-8) + 0.1 * w
    return (w - 0.02 * step).astype(BF), m, v


def params(axes, **more):
    return pltpu.CompilerParams(dimension_semantics=("arbitrary",) * axes, vmem_limit_bytes=VMEM, **more)


def cost(flops, bytes_):
    return pl.CostEstimate(flops=flops, bytes_accessed=bytes_, transcendentals=0)


def hidden(a, wg, wu, tm=512, tn=1408):
    tokens, d = a.shape
    n = wg.shape[1]

    def kernel(a, g, u, o):
        gate, up = dot(a[...], whole(g), TB), dot(a[...], whole(u), TB)
        o[...] = (gate * jax.nn.sigmoid(gate) * up).astype(BF)

    w = pl.BlockSpec((4, tn, d // 4), lambda n, m: (0, n, 0))
    return pl.pallas_call(
        kernel,
        out_shape=jax.ShapeDtypeStruct((tokens, n), BF),
        grid=(n // tn, tokens // tm),
        in_specs=[pl.BlockSpec((tm, d), lambda n, m: (m, 0)), w, w],
        out_specs=pl.BlockSpec((tm, tn), lambda n, m: (m, n)),
        compiler_params=params(2),
        cost_estimate=cost(4 * tokens * d * n, 2 * tokens * (d + n)),
        name="hidden",
    )(a, wg, wu)


def down(p, wd, h, tm=512):
    tokens, n = p.shape
    d = h.shape[1]

    def kernel(p, w, h, ho, ao):
        new = h[...] + dot(p[...], w[...], NN).astype(BF)
        ho[...] = new
        ao[...] = normed(new)

    row = pl.BlockSpec((tm, d), lambda m: (m, 0))
    return pl.pallas_call(
        kernel,
        out_shape=(jax.ShapeDtypeStruct((tokens, d), BF),) * 2,
        grid=(tokens // tm,),
        in_specs=[pl.BlockSpec((tm, n), lambda m: (m, 0)), pl.BlockSpec((n, d), lambda m: (0, 0)), row],
        out_specs=(row, row),
        compiler_params=params(1),
        cost_estimate=cost(2 * tokens * d * n, 2 * tokens * (3 * d + n)),
        name="down",
    )(p, wd, h)


def inner(a, dy, wg, wu, wd, tm=512, tn=704):
    tokens, d = a.shape
    n = wd.shape[0]

    def kernel(a, dy, g, u, w, o):
        gate, up = dot(whole(g), a[...], TB), dot(whole(u), a[...], TB)
        by_p = dot(w[...], dy[...], TB).astype(BF).astype(F32)
        sig = jax.nn.sigmoid(gate)
        act = gate * sig
        o[0] = (act * up).astype(BF)
        o[1] = (by_p * up * (sig * (1.0 + gate * (1.0 - sig)))).astype(BF)
        o[2] = (by_p * act).astype(BF)

    w = pl.BlockSpec((4, tn, d // 4), lambda n, m: (0, n, 0))
    act = pl.BlockSpec((tm, d), lambda n, m: (m, 0))
    return pl.pallas_call(
        kernel,
        out_shape=jax.ShapeDtypeStruct((3, n, tokens), BF),
        grid=(n // tn, tokens // tm),
        in_specs=[act, act, w, w, pl.BlockSpec((tn, d), lambda n, m: (n, 0))],
        out_specs=pl.BlockSpec((3, tn, tm), lambda n, m: (0, n, m)),
        compiler_params=params(2),
        cost_estimate=cost(6 * tokens * d * n, 2 * tokens * (2 * d + 3 * n)),
        name="inner",
    )(a, dy, wg, wu, wd)


def below(x, wg, wu, h, dh, tm=256):
    tokens, d = h.shape
    n = x.shape[1]

    def kernel(x, g, u, h, dh, o):
        by_a = dot(x[0], whole(g), TA).astype(BF).astype(F32) + dot(x[1], whole(u), TA).astype(BF).astype(F32)
        wide = h[...].astype(F32)
        r = scale_of(wide)
        by_h = by_a * r - wide * (r * r * r) * jnp.mean(by_a * wide, -1, keepdims=True)
        o[...] = dh[...] + by_h.astype(BF)

    row = pl.BlockSpec((tm, d), lambda m: (m, 0))
    w = pl.BlockSpec((4, n, d // 4), lambda m: (0, 0, 0))

    def two(x_gate, x_up, g, u, h, dh, o):
        kernel((x_gate[0], x_up[0]), g, u, h, dh, o)

    return pl.pallas_call(
        two,
        out_shape=jax.ShapeDtypeStruct((tokens, d), BF),
        grid=(tokens // tm,),
        in_specs=[pl.BlockSpec((1, n, tm), lambda m: (1, 0, m)), pl.BlockSpec((1, n, tm), lambda m: (2, 0, m)), w, w, row, row],
        out_specs=row,
        compiler_params=params(1),
        cost_estimate=cost(4 * tokens * d * n, 2 * tokens * (3 * d + 2 * n)),
        name="below",
    )(x, x, wg, wu, h, dh)


LAG = (0, 1, 3, 5, 7)
ROWS = 64


def summed(xs, rights):
    _, n, tokens = xs[0].shape
    d = rights[0][0].shape[1]
    quarter = n // 4
    per = quarter // ROWS
    layers = len(xs)
    chunks = layers * 3 * per
    wide = d // 4
    slots = 4

    def kernel(*refs):
        x_refs, r_refs = refs[:layers], refs[layers : 3 * layers]
        out, right, acc, csend, crecv, mine, xsend, xrecv, ysend, yrecv, zsend, zrecv, rsem, csems, xsems, ysems, zsems = refs[3 * layers :]
        t = pl.program_id(0)
        s, r = lax.axis_index("s"), lax.axis_index("r")
        core, x, y, z = s % 2, s // 2, r // 2, r % 2
        other, over_x, over_y, over_z = s + 1 - 2 * core, s + 2 - 4 * x, r + 2 - 4 * y, r + 1 - 2 * z

        def load(i):
            return pltpu.make_async_copy(r_refs[i], right.at[i % 2], rsem.at[i % 2])

        def send(src, dst, sems, slot, to):
            return pltpu.make_async_remote_copy(
                src_ref=src.at[slot], dst_ref=dst.at[slot], send_sem=sems.at[0, slot], recv_sem=sems.at[1, slot],
                device_id=to, device_id_type=MESH,
            )

        def along_core(u):
            return send(csend, crecv, csems, u % 2, {"s": other})

        def along_x(u):
            return send(xsend, xrecv, xsems, u % slots, {"s": over_x})

        def along_y(u):
            return send(ysend, yrecv, ysems, u % slots, {"r": over_y})

        def along_z(u):
            return send(zsend, zrecv, zsems, u % slots, {"r": over_z})

        @pl.when(t == 0)
        def _():
            load(0).start()
            load(1).start()
            barrier = pltpu.get_barrier_semaphore()
            for to in ({"s": other}, {"s": over_x}, {"r": over_y}, {"r": over_z}):
                pl.semaphore_signal(barrier, inc=1, device_id=to, device_id_type=MESH)
            pl.semaphore_wait(barrier, 4)

        for layer in range(layers):
            first = layer * 3 * per

            @pl.when(t == first)
            def _():
                load(2 * layer).wait()
                if layer:
                    load(2 * layer + 1).start()

            @pl.when(t == first + per)
            def _():
                load(2 * layer + 1).wait()
                if layer + 1 < layers:
                    load(2 * layer + 2).start()

            @pl.when((t >= first) & (t < first + per))
            def _():
                o = dot(x_refs[layer][...].reshape(4 * ROWS, tokens), right[0], NN)
                for q in range(4):
                    acc[t % 2, q] = o[ROWS * q : ROWS * (q + 1)]

            @pl.when((t >= first + per) & (t < first + 3 * per))
            def _():
                o = dot(x_refs[layer][...].reshape(4 * ROWS, tokens), right[1], NN)
                for q in range(4):
                    for p in range(4):
                        acc[t % 2, p, :, wide * q : wide * (q + 1)] = o[ROWS * q : ROWS * (q + 1), wide * p : wide * (p + 1)]

        @pl.when(t >= LAG[4])
        def _():
            u = t - LAG[4]
            along_z(u).wait()
            out[0] = (zsend[u % slots].astype(F32) + zrecv[u % slots].astype(F32)).astype(BF)

        @pl.when((t >= LAG[3]) & (t < chunks + LAG[3]))
        def _():
            u = t - LAG[3]
            along_y(u).wait()
            zsend[u % slots] = (ysend[u % slots].astype(F32) + yrecv[u % slots].astype(F32)).astype(BF)
            along_z(u).start()

        @pl.when((t >= LAG[2]) & (t < chunks + LAG[2]))
        def _():
            u = t - LAG[2]
            along_x(u).wait()
            ysend[u % slots] = (mine[u % slots] + xrecv[u % slots].astype(F32)).astype(BF)
            along_y(u).start()

        @pl.when((t >= LAG[1]) & (t < chunks + LAG[1]))
        def _():
            u = t - LAG[1]
            along_core(u).wait()
            xsend[u % slots] = (acc[u % 2, 2 - 2 * x + core] + crecv[u % 2, 1 - x].astype(F32)).astype(BF)
            along_x(u).start()
            mine[u % slots] = acc[u % 2, 2 * x + core] + crecv[u % 2, x].astype(F32)

        @pl.when(t < chunks)
        def _():
            for j in range(2):
                csend[t % 2, j] = acc[t % 2, 2 * j + 1 - core].astype(BF)
            along_core(t).start()

    def lhs(layer):
        def index(t):
            u = jnp.clip(t - layer * 3 * per, 0, 3 * per - 1)
            return u // per, 0, u % per, 0

        return pl.BlockSpec((1, 4, ROWS, tokens), index)

    block = (ROWS, d)
    dma = pltpu.SemaphoreType.DMA
    return pl.pallas_call(
        kernel,
        out_shape=jax.ShapeDtypeStruct((chunks,) + block, BF),
        grid=(chunks + LAG[4],),
        in_specs=[lhs(layer) for layer in range(layers)] + [pl.BlockSpec(memory_space=pl.ANY)] * (2 * layers),
        out_specs=pl.BlockSpec((1,) + block, lambda t: (jnp.maximum(t - LAG[4], 0), 0, 0)),
        scratch_shapes=[
            pltpu.VMEM((2, tokens, d), BF),
            pltpu.VMEM((2, 4) + block, F32),
            pltpu.VMEM((2, 2) + block, BF),
            pltpu.VMEM((2, 2) + block, BF),
            pltpu.VMEM((slots,) + block, F32),
        ]
        + [pltpu.VMEM((slots,) + block, BF)] * 6
        + [dma((2,)), dma((2, 2)), dma((2, slots)), dma((2, slots)), dma((2, slots))],
        compiler_params=params(1, collective_id=0, has_side_effects=True),
        cost_estimate=cost(2 * chunks * 4 * ROWS * tokens * d, 2 * layers * tokens * (3 * n + 2 * d)),
        name="summed",
    )(*[x.reshape(3, 4, quarter, tokens) for x in xs], *[r for pair in rights for r in pair])


def solution(mesh):
    def step(x, dy, *arrays):
        weights, m, v = (arrays[i : i + 3] for i in (0, 3, 6))
        layers = weights[0].shape[0]

        def fetched(number):
            gate, up = (lax.all_gather(w[number].T, "s", axis=0) for w in weights[:2])
            return gate, up, lax.all_gather(weights[2][number], "s", axis=0, tiled=True)

        full = [fetched(number) for number in range(layers)]
        h, kept = x[0], []
        a = normed(h)
        for number in range(layers):
            kept.append((h, a))
            if number + 1 < layers:
                gate, up, wd = full[number]
                h, a = down(hidden(a, gate, up), wd, h)
        by_h = dy[0]
        xs, rights = [], []
        for number in reversed(range(layers)):
            gate, up, wd = full[number]
            h, a = kept[number]
            xs.append(inner(a, by_h, gate, up, wd))
            rights.append((by_h, a))
            if number:
                by_h = below(xs[-1], gate, up, h, by_h)
        g = summed(xs, rights)
        g = g.reshape(layers, 3, -1, ROWS, g.shape[-1])[::-1]
        quarter = g.shape[2] * ROWS
        by_down = g[:, 0].reshape(layers, quarter, -1)

        def turned(g):
            g = g.reshape(layers, -1, ROWS, 4, g.shape[-1] // 4)
            return g.transpose(0, 4, 3, 1, 2).reshape(layers, g.shape[-1], 4 * quarter)

        gradients = [turned(g[:, 1]), turned(g[:, 2]), by_down]
        new = [adamw(w.astype(F32), m, v, g.astype(F32)) for w, m, v, g in zip(weights, m, v, gradients, strict=True)]
        return tuple(one[which] for which in range(3) for one in new)

    states, cut = P(("rep", "r", "s"), None, None), P(None, "s", None)
    return jax.shard_map(
        step,
        mesh=mesh,
        in_specs=(states, states) + (cut,) * 9,
        out_specs=(P("rep", "s", None),) * 9,
        check_vma=False,
    )
```

time: 989 us -> 868 us (0.88)
  matrix products: 573 us -> 0 us
  Pallas kernels: 0 us -> 557 us
  waiting for transfers between devices: 311 us -> 99.4 us
  local copies, waits for them, and re-layouts: 33.9 us -> 140 us
    dot_general x15 -> x0, matrix products: 573 us -> none  [the longest x5 203 us: layer(): up = jnp.dot(a, w['w_up'], preferred_element_type=jnp.float32)]
    pallas_call x0 -> x6, Pallas kernels: none -> 557 us  [the longest x1 210 us: summed(): pl.pallas_call(kernel, out_shape=jax.ShapeDtypeStruct((chunks,) + block,...]
    psum x1 -> x0, waiting for transfers between devices: 173 us -> none  [summed(): lax.psum(lax.psum_scatter(term, 's', scatter_dimension=0, tiled=True), 'r')]
    reduce_scatter x6 -> x0, waiting for transfers between devices: 94.5 us -> none  [summed(): lax.psum_scatter(term, 's', scatter_dimension=0, tiled=True)]
    all_gather x6, waiting for transfers between devices: 42.1 us -> 97.6 us  [the longest x4 97.6 us: fetched(): gate, up = (lax.all_gather(w[number].T, 's', axis=0) for w in weights[:2])]
    unnamed x32 -> x30, local copies, waits for them, and re-layouts: 24.8 us -> 66.6 us
    all_gather x0 -> x4, local copies, waits for them, and re-layouts: none -> 33.2 us  [fetched(): gate, up = (lax.all_gather(w[number].T, 's', axis=0) for w in weights[:2])]
    convert_element_type x0 -> x4, local copies, waits for them, and re-layouts: none -> 23.6 us  [step(): g.astype(F32)]
  transfers between devices with their start and end apart: 13 -> 6, of which waited for: 7 -> 3; matrix products, arithmetic and copies ran while one was open for 45% -> 10% of each run, Pallas kernels for 0% -> 11%
where the time goes in v1:
time: 868 us; the launch traced here: 857 us
  Pallas kernels  557 us (64%)
  local copies, waits for them, and re-layouts  140 us (16%)
  waiting for transfers between devices  99.4 us (11%)
  other arithmetic  46.5 us (5%)
  between operations  14.7 us (2%)
    pallas_call x1, Pallas kernels, summed(): pl.pallas_call(kernel, out_shape=jax.ShapeDtypeStruct((chunks,) + block,...  210 us
    pallas_call x2, Pallas kernels, inner(): pl.pallas_call(kernel, out_shape=jax.ShapeDtypeStruct((3, n, tokens), BF)...  192 us
    all_gather x4, waiting for transfers between devices, fetched(): gate, up = (lax.all_gather(w[number].T, 's', axis=0) for w in weights[:2])  97.6 us
    unnamed x30, local copies, waits for them, and re-layouts  66.6 us
    pallas_call x1, Pallas kernels, below(): pl.pallas_call(two, out_shape=jax.ShapeDtypeStruct((tokens, d), BF), grid...  62.1 us
    pallas_call x1, Pallas kernels, hidden(): pl.pallas_call(kernel, out_shape=jax.ShapeDtypeStruct((tokens, n), BF), g...  60.3 us
    all_gather x4, local copies, waits for them, and re-layouts, fetched(): gate, up = (lax.all_gather(w[number].T, 's', axis=0) for w in weights[:2])  33.2 us
    pallas_call x1, Pallas kernels, down(): pl.pallas_call(kernel, out_shape=(jax.ShapeDtypeStruct((tokens, d), BF),)...  32.5 us
  transfers between devices with their start and end apart: 6, of which 3 were waited for; matrix products, arithmetic and copies ran while one was open for 10% of the time, Pallas kernels for 11%

profile of v1, /device:TPU:0, one launch (start us, length us, event | category | flops | bytes accessed | tf_op | source)
XLA Modules:
  0.0 857.2 jit_solution(13314940413756543777)
XLA Ops:
  7.2 0.0 copy-start
  7.2 0.0 all-gather.13.cloned.1.call-start
  7.2 3.7 slice_bitcast_fusion.3
  10.9 0.0 all-gather.13.cloned.1.call-update
  11.0 0.0 all-gather.15.cloned.1.call-start
  11.0 0.0 copy-done
  11.0 1.8 slice_bitcast_fusion.2
  12.8 0.0 all-gather.15.cloned.1.call-update
  12.8 0.0 all-gather.19.cloned.1.call-start
  12.9 0.7 all-gather.19.cloned.1.call-update
  13.5 0.0 all-gather.21.cloned.1.call-start
  13.6 0.5 all-gather.21.cloned.1.call-update
  14.1 0.0 all-gather.17.cloned.1.call-start
  14.2 3.6 fusion.24
  17.8 0.0 all-gather.17.cloned.1.call-update
  17.8 0.0 all-gather.23.cloned.1.call-start
  17.9 0.5 all-gather.23.cloned.1.call-update
  18.4 2.7 copy.51
  21.1 4.5 copy.42
  25.7 6.2 copy.52
  31.9 6.3 copy.55
  38.2 6.2 copy.43
  44.4 6.2 copy.50
  50.6 5.1 fusion
  55.7 8.0 fusion.1.a.refs_5_
  63.7 0.0 all-gather.13.cloned.1.call-done
  63.7 8.3 copy.44
  72.0 27.0 %all-gather.15.cloned.1.call-done = bf16[11264,256]{0,1:T(8,128)(2,1)} async-done(((bf16[2816,256]{0,1:T(8,128)(2,1)}), bf16[11264,256]{0,1:T(8,128)(2,1)}) %all-gather.15.cloned.1.call-update) | async-done | bytes 5767184 | tf_op jit(solution)/shard_map/all_gather | solution.py:298
  99.1 8.3 copy.45
  107.4 35.3 %all-gather.19.cloned.1.call-done = bf16[11264,256]{0,1:T(8,128)(2,1)} async-done(((bf16[2816,256]{0,1:T(8,128)(2,1)}), bf16[11264,256]{0,1:T(8,128)(2,1)}) %all-gather.19.cloned.1.call-update) | async-done | bytes 5767184 | tf_op jit(solution)/shard_map/all_gather | solution.py:298
  142.7 8.3 copy.46
  151.0 35.2 %all-gather.21.cloned.1.call-done = bf16[11264,256]{0,1:T(8,128)(2,1)} async-done(((bf16[2816,256]{0,1:T(8,128)(2,1)}), bf16[11264,256]{0,1:T(8,128)(2,1)}) %all-gather.21.cloned.1.call-update) | async-done | bytes 5767184 | tf_op jit(solution)/shard_map/all_gather | solution.py:298
  186.2 8.3 copy.47
  194.5 60.3 %hidden.1.p = bf16[4096,2816]{1,0:T(8,128)(2,1)} custom-call(bf16[4096,1024]{1,0:T(8,128)(2,1)} %fusion.1.a.refs_5_, bf16[4,2816,256]{2,1,0:T(8,128)(2,1)} %bitcast.78, bf16[4,2816,256]{2,1,0:T(8,128)(2,1)} %bitcast.80), custom_call_target="tpu_custom_call" | custom-call | flops 47244640256 | bytes 31457280 | tf_op jit(solution)/shard_map/hidden/pallas_call | solution.py:58
  254.8 0.0 all-gather.17.cloned.1.call-done
  254.8 32.5 %down.1 = (bf16[4096,1024]{1,0:T(8,128)(2,1)}, bf16[4096,1024]{1,0:T(8,128)(2,1)}) custom-call(bf16[4096,2816]{1,0:T(8,128)(2,1)} %hidden.1.p, bf16[2816,1024]{1,0:T(8,128)(2,1)} %bitcast.82, bf16[4096,1024]{1,0:T(8,128)(2,1)} %bitcast.63), custom_call_target="tpu_custom_call" | custom-call | flops 23622320128 | bytes 48234496 | tf_op jit(solution)/shard_map/down/pallas_call | solution.py:80
  287.3 95.9 %inner.2.x_gate.x_up = bf16[3,2816,4096]{2,1,0:T(8,128)(2,1)} custom-call(bf16[4096,1024]{1,0:T(8,128)(2,1)} %get-tuple-element.11.a.refs_3_, bf16[4096,1024]{1,0:T(8,128)(2,1)} %bitcast.75, bf16[4,2816,256]{2,1,0:T(8,128)(2,1)} %bitcast.70, bf16[4,2816,256]{2,1,0:T(8,128)(2,1)} %bitcast.72, bf16[2816,1024]{1,0:T(8,128)(2,1)} %bitcast.84), custom_call_target="tpu_custom_call" | custom-call | flops 70866960384 | bytes 85983232 | tf_op jit(solution)/shard_map/inner/pallas_call | solution.py:107
  383.2 62.1 %below.1.dy.refs_4_ = bf16[4096,1024]{1,0:T(8,128)(2,1)} custom-call(bf16[3,2816,4096]{2,1,0:T(8,128)(2,1)} %inner.2.x_gate.x_up, bf16[3,2816,4096]{2,1,0:T(8,128)(2,1)} %inner.2.x_gate.x_up, bf16[4,2816,256]{2,1,0:T(8,128)(2,1)} %bitcast.71, bf16[4,2816,256]{2,1,0:T(8,128)(2,1)} %bitcast.73, bf16[4096,1024]{1,0:T(8,128)(2,1)} %get-tuple-element.12.h, ...), custom_call_target="tpu_custom_call" | custom-call | flops 47244640256 | bytes 71303168 | tf_op jit(solution)/shard_map/below/pallas_call | solution.py:136
  445.3 95.7 %inner.3 = bf16[3,2816,4096]{2,1,0:T(8,128)(2,1)} custom-call(bf16[4096,1024]{1,0:T(8,128)(2,1)} %fusion.1.a.refs_5_, bf16[4096,1024]{1,0:T(8,128)(2,1)} %below.1.dy.refs_4_, bf16[4,2816,256]{2,1,0:T(8,128)(2,1)} %bitcast.79, bf16[4,2816,256]{2,1,0:T(8,128)(2,1)} %bitcast.81, bf16[2816,1024]{1,0:T(8,128)(2,1)} %bitcast.83), custom_call_target="tpu_custom_call" | custom-call | flops 70866960384 | bytes 85983232 | tf_op jit(solution)/shard_map/inner/pallas_call | solution.py:107
  541.0 210.3 %summed.1 = bf16[66,64,1024]{2,1,0:T(8,128)(2,1)} custom-call(bf16[3,4,704,4096]{3,2,1,0:T(8,128)(2,1)} %bitcast.16.refs_0_, bf16[3,4,704,4096]{3,2,1,0:T(8,128)(2,1)} %bitcast.17.refs_1_, bf16[4096,1024]{1,0:T(8,128)(2,1)} %bitcast.77, bf16[4096,1024]{1,0:T(8,128)(2,1)} %get-tuple-element.11.a.refs_3_, bf16[4096,1024]{1,0:T(8,128)(2,1)} %below.1.dy.refs_4_, ...), custom_call_target="tpu_custom_call" | custom-call | flops 141733920768 | bytes 171966464 | tf_op jit(solution)/shard_map/summed/pallas_call | solution.py:271
  751.4 5.2 fusion.23
  756.5 5.8 reverse_convert_fusion
  762.3 7.9 reshape.54
  770.2 3.9 copy.54
  774.1 0.0 slice-done.2
  774.1 0.0 slice-done.3
  774.1 0.9 copy-done.2
  775.0 8.2 fusion.7
  783.2 6.2 copy.59
  789.4 6.4 copy.61
  795.7 0.0 copy-done.4
  795.8 2.9 copy.57
  798.7 7.9 reshape.53
  806.6 3.9 copy.49
  810.5 0.0 slice-done
  810.5 0.0 slice-done.1
  810.5 0.9 copy-done.1
  811.4 7.9 fusion.4
  819.3 6.2 copy.58
  825.5 6.2 copy.60
  831.8 4.7 copy.56
  836.5 0.0 copy-done.3
  836.5 2.0 slice.47
  838.4 11.5 %fusion.10 = (bf16[2,704,1024]{2,1,0:T(8,128)(2,1)}, f32[2,704,1024]{2,1,0:T(8,128)}, f32[2,704,1024]{2,1,0:T(8,128)}) fusion(bf16[2,704,1024]{2,1,0:T(8,128)(2,1)} %param.15, bf16[2,1,11,64,1024]{4,3,2,1,0:T(8,128)(2,1)} %slice.47, f32[2,704,1024]{2,1,0:T(8,128)} %param.21, f32[2,704,1024]{2,1,0:T(8,128)} %param.18), kind=kLoop, calls=%fused_computation.23 | loop fusion | flops 23068672 | bytes 31719424 | tf_op jit(solution)/shard_map/convert_element_type | solution.py:38
  (12 shorter events, 0.0 us)
Async XLA Ops:
  7.2 3.8 copy-start
  7.2 56.6 %all-gather.13.cloned.1.call-start = ((), (), s32[]{:S(2)}) async-start(), calls=%async_computation | async-start | bytes 7208960 | tf_op jit(solution)/shard_map/all_gather | solution.py:298
  11.0 88.1 %all-gather.15.cloned.1.call-start = ((), (), s32[]{:S(2)}) async-start(), calls=%async_computation.1 | async-start | bytes 7208960 | tf_op jit(solution)/shard_map/all_gather | solution.py:298
  12.8 129.9 %all-gather.19.cloned.1.call-start = ((), (), s32[]{:S(2)}) async-start(), calls=%async_computation.3 | async-start | bytes 7208960 | tf_op jit(solution)/shard_map/all_gather | solution.py:298
  13.5 172.7 %all-gather.21.cloned.1.call-start = ((), (), s32[]{:S(2)}) async-start(), calls=%async_computation.4 | async-start | bytes 7208960 | tf_op jit(solution)/shard_map/all_gather | solution.py:298
  14.1 240.7 %all-gather.17.cloned.1.call-start = ((), (), s32[]{:S(2)}) async-start(), calls=%async_computation.2 | async-start | bytes 7208960 | tf_op jit(solution)/shard_map/all_gather | solution.py:299
  17.8 269.5 %all-gather.23.cloned.1.call-start = ((), (), s32[]{:S(2)}) async-start(), calls=%async_computation.5 | async-start | bytes 7208960 | tf_op jit(solution)/shard_map/all_gather | solution.py:299
  762.3 11.8 %slice-start.2 = ((s8[5767168]{0:T(1024)(128)(4,1)}), s8[1572864]{0:T(1024)(128)(4,1)S(1)}, s32[]{:S(2)}) async-start(s8[5767168]{0:T(1024)(128)(4,1)} %bitcast.68), calls=%async_computation.8 | async-start | bytes 3145728
  770.2 3.9 slice-start.3
  770.2 4.8 copy-start.2
  789.4 6.4 copy-start.4
  798.7 11.8 %slice-start = ((s8[5767168]{0:T(1024)(128)(4,1)}), s8[1572864]{0:T(1024)(128)(4,1)S(1)}, s32[]{:S(2)}) async-start(s8[5767168]{0:T(1024)(128)(4,1)} %bitcast.66), calls=%async_computation.6 | async-start | bytes 3145728
  806.6 3.9 slice-start.1
  806.6 4.8 copy-start.1
  831.8 4.7 copy-start.3
Sparse Core Ops, SparseCore 0:
  11.1 44.3 all-gather.12
  57.6 41.4 all-gather.14
  101.2 41.4 all-gather.18
  144.7 41.4 all-gather.20
  187.6 41.4 all-gather.16
  230.5 41.4 all-gather.22

commit v2 on v1

--- a/solution.py
+++ b/solution.py
@@ -46,28 +46,228 @@
     return pl.CostEstimate(flops=flops, bytes_accessed=bytes_, transcendentals=0)
 
 
-def hidden(a, wg, wu, tm=512, tn=1408):
-    tokens, d = a.shape
-    n = wg.shape[1]
-
-    def kernel(a, g, u, o):
-        gate, up = dot(a[...], whole(g), TB), dot(a[...], whole(u), TB)
-        o[...] = (gate * jax.nn.sigmoid(gate) * up).astype(BF)
-
-    w = pl.BlockSpec((4, tn, d // 4), lambda n, m: (0, n, 0))
+def started(x, w_gate, w_up, w_down, tm=512, tn=1408):
+    tokens, d = x.shape
+    layers, wide, n = w_gate.shape
+    quarter = n // 4
+    steps_m = tokens // tm
+    last = (n // tn) * steps_m
+
+    def kernel(x_ref, g_ref, u_ref, d_ref, p_ref, a_ref, fg, fu, fd, a, g0, u0, turned, flat, dv, sems, local):
+        t = pl.program_id(0) * steps_m + pl.program_id(1)
+        s, r = lax.axis_index("s"), lax.axis_index("r")
+        core, px, py, pz = s % 2, s // 2, r // 2, r % 2
+        sx = s + 2 - 4 * px
+        to_core, to_x = {"s": s + 1 - 2 * core}, {"s": sx}
+        to_y, to_z = {"r": r + 2 - 4 * py}, {"r": r + 1 - 2 * pz}
+
+        def item(number, own, full, base, size, by):
+            def copy(kind, src, dst, to):
+                return pltpu.make_async_remote_copy(
+                    src_ref=src, dst_ref=dst, send_sem=sems.at[0, number, kind], recv_sem=sems.at[1, number, kind],
+                    device_id=to, device_id_type=MESH,
+                )
+
+            def relay(kind, rows, to):
+                return copy(kind, full(sx, rows), full(sx, rows), to)
+
+            every = pl.ds(base, size)
+            if by in ("y", "z"):
+                half = size // 2
+                par = py if by == "y" else pz
+                mine, theirs = pl.ds(base + par * half, half), pl.ds(base + (1 - par) * half, half)
+                out = {
+                    "x": copy(0, own(mine), full(s, mine), to_x),
+                    "r": relay(2, mine, to_y if by == "y" else to_z),
+                    "cx": relay(3, mine, to_core),
+                    "cr": relay(4, theirs, to_core),
+                }
+            else:
+                part = size // 4
+
+                def at(y, z):
+                    return pl.ds(base + (2 * y + z) * part, part)
+
+                mine = at(py, pz)
+                out = {
+                    "x": copy(0, own(mine), full(s, mine), to_x),
+                    "y": relay(2, mine, to_y),
+                    "z": relay(3, mine, to_z),
+                    "cx": relay(4, mine, to_core),
+                    "cy": relay(5, at(1 - py, pz), to_core),
+                    "cz": relay(6, at(py, 1 - pz), to_core),
+                    "d": relay(7, at(1 - py, pz), to_z) if by == "yz" else relay(7, at(py, 1 - pz), to_y),
+                    "cd": relay(8, at(1 - py, 1 - pz), to_core),
+                }
+            out["c"] = copy(1, own(every), full(s, every), to_core)
+            return out
+
+        def inside(ref):
+            return (lambda rows: ref.at[s, rows]), (lambda block, rows: ref.at[block, rows])
+
+        def outside(own, ref):
+            return (lambda rows: own.at[rows]), (lambda block, rows: ref.at[1, block, rows])
+
+        g0a, u0a = item(0, *inside(g0), 0, tn, "y"), item(1, *inside(u0), 0, tn, "z")
+        g0b, u0b = item(2, *inside(g0), tn, tn, "y"), item(3, *inside(u0), tn, tn, "z")
+        d0 = item(4, lambda rows: d_ref.at[0, rows], lambda block, rows: fd.at[0, block, rows], 0, quarter, "yz")
+        g1 = item(5, *outside(turned.at[0], fg), 0, n, "zy")
+        u1 = item(6, *outside(turned.at[1], fu), 0, n, "yz")
+        d1 = item(7, lambda rows: d_ref.at[1, rows], lambda block, rows: fd.at[1, block, rows], 0, quarter, "zy")
+        items = (g0a, u0a, g0b, u0b, d0, g1, u1, d1)
+
+        def here(k, src, dst):
+            return pltpu.make_async_copy(src, dst, local.at[k])
+
+        loads = [here(2 * i + j, ref.at[i], flat.at[2 * i + j]) for i in range(2) for j, ref in enumerate((g_ref, u_ref))]
+        load_x, load_d = here(4, x_ref, a), here(5, d_ref, dv)
+        keep = [
+            here(6, turned.at[0], fg.at[1, s]),
+            here(7, turned.at[1], fu.at[1, s]),
+            here(8, dv.at[0], fd.at[0, s]),
+            here(9, dv.at[1], fd.at[1, s]),
+            here(10, a, a_ref),
+            here(11, g0, fg.at[0]),
+            here(12, u0, fu.at[0]),
+        ]
+
+        def begin(one):
+            one["x"].start()
+            one["c"].start()
+
+        def got(one, *kinds):
+            for kind in kinds:
+                one[kind].wait_recv()
+
+        def go(one, *kinds):
+            for kind in kinds:
+                one[kind].start()
+
+        @pl.when(t == 0)
+        def _():
+            for load in (*loads[:2], load_x, load_d, *loads[2:]):
+                load.start()
+            barrier = pltpu.get_barrier_semaphore()
+            for to in (to_core, to_x, to_y, to_z):
+                pl.semaphore_signal(barrier, inc=1, device_id=to, device_id_type=MESH)
+            pl.semaphore_wait(barrier, 4)
+            loads[0].wait()
+            loads[1].wait()
+            for base, pair in ((0, (g0a, u0a)), (tn, (g0b, u0b))):
+                for j, (ref, one) in enumerate(zip((g0, u0), pair, strict=True)):
+                    ref[s, base : base + tn] = flat[j, :, base : base + tn].T
+                    begin(one)
+            begin(d0)
+            load_x.wait()
+
+            @pl.loop(0, steps_m)
+            def _(i):
+                rows = pl.ds(i * tm, tm)
+                a[rows, :] = normed(a[rows, :])
+
+            keep[4].start()
+            got(g0a, "x")
+            go(g0a, "r", "cx")
+            for j, one in enumerate((g1, u1)):
+                loads[2 + j].wait()
+                for base in (0, tn):
+                    turned[j, base : base + tn] = flat[2 + j, :, base : base + tn].T
+                begin(one)
+                keep[j].start()
+            begin(d1)
+            load_d.wait()
+            keep[2].start()
+            keep[3].start()
+            got(u0a, "x")
+            go(u0a, "r", "cx")
+            got(g0a, "r")
+            go(g0a, "cr")
+            got(u0a, "r")
+            go(u0a, "cr")
+            got(g0a, "c", "cx", "cr")
+            got(u0a, "c", "cx", "cr")
+
+        def on(step, *todo):
+            @pl.when(t == step)
+            def _():
+                for one, wait, then in todo:
+                    got(one, *wait)
+                    go(one, *then)
+
+        on(1, (g0b, ("x",), ("r", "cx")))
+        on(3, (u0b, ("x",), ("r", "cx")))
+        on(4, (g0b, ("r",), ("cr",)))
+        on(5, (d0, ("x",), ("y", "z", "cx")))
+        on(6, (u0b, ("r",), ("cr",)))
+        on(7, (g1, ("x",), ("y", "z", "cx")))
+
+        @pl.when(t == steps_m)
+        def _():
+            got(g0b, "c", "cx", "cr")
+            got(u0b, "c", "cx", "cr")
+            keep[5].start()
+            keep[6].start()
+
+        on(8, (d0, ("y", "z"), ("cy", "cz", "d")))
+        on(9, (u1, ("x",), ("y", "z", "cx")))
+        on(10, (g1, ("y", "z"), ("cy", "cz", "d")))
+        on(11, (d1, ("x",), ("y", "z", "cx")), (d0, ("d",), ("cd",)))
+        on(12, (u1, ("y", "z"), ("cy", "cz", "d")))
+        on(13, (g1, ("d",), ("cd",)))
+        on(14, (d1, ("y", "z"), ("cy", "cz", "d")))
+        on(15, (u1, ("d",), ("cd",)))
+
+        rows = pl.ds(pl.program_id(1) * tm, tm)
+        columns = pl.ds(pl.program_id(0) * tn, tn)
+        block = a[rows, :]
+        gate = dot(block, whole([g0[q, columns] for q in range(4)]), TB)
+        up = dot(block, whole([u0[q, columns] for q in range(4)]), TB)
+        p_ref[...] = (gate * jax.nn.sigmoid(gate) * up).astype(BF)
+
+        @pl.when(t == last - 1)
+        def _():
+            got(d1, "d")
+            go(d1, "cd")
+            for one in (d0, g1, u1, d1):
+                got(one, "c", "cx", "cy", "cz", "cd")
+            for one in items:
+                for copy in one.values():
+                    copy.wait_send()
+            for copy in keep:
+                copy.wait()
+
+    hbm = pl.BlockSpec(memory_space=pl.ANY)
+    dma = pltpu.SemaphoreType.DMA
+    full = jax.ShapeDtypeStruct((layers, 4, n, wide), BF)
     return pl.pallas_call(
         kernel,
-        out_shape=jax.ShapeDtypeStruct((tokens, n), BF),
-        grid=(n // tn, tokens // tm),
-        in_specs=[pl.BlockSpec((tm, d), lambda n, m: (m, 0)), w, w],
-        out_specs=pl.BlockSpec((tm, tn), lambda n, m: (m, n)),
-        compiler_params=params(2),
+        out_shape=(
+            jax.ShapeDtypeStruct((tokens, n), BF),
+            jax.ShapeDtypeStruct((tokens, d), BF),
+            full,
+            full,
+            jax.ShapeDtypeStruct((layers, 4, quarter, d), BF),
+        ),
+        grid=(n // tn, steps_m),
+        in_specs=[hbm] * 4,
+        out_specs=(pl.BlockSpec((tm, tn), lambda n, m: (m, n)), hbm, hbm, hbm, hbm),
+        scratch_shapes=[
+            pltpu.VMEM((tokens, d), BF),
+            pltpu.VMEM((4, n, wide), BF),
+            pltpu.VMEM((4, n, wide), BF),
+            pltpu.VMEM((2, n, wide), BF),
+            pltpu.VMEM((4, wide, n), BF),
+            pltpu.VMEM((layers, quarter, d), BF),
+            dma((2, 8, 9)),
+            dma((13,)),
+        ],
+        compiler_params=params(2, collective_id=1, has_side_effects=True),
         cost_estimate=cost(4 * tokens * d * n, 2 * tokens * (d + n)),
-        name="hidden",
-    )(a, wg, wu)
-
-
-def down(p, wd, h, tm=512):
+        name="started",
+    )(x, w_gate, w_up, w_down)
+
+
+def down(p, wd, layer, h, tm=512):
     tokens, n = p.shape
     d = h.shape[1]
 
@@ -81,7 +281,7 @@
         kernel,
         out_shape=(jax.ShapeDtypeStruct((tokens, d), BF),) * 2,
         grid=(tokens // tm,),
-        in_specs=[pl.BlockSpec((tm, n), lambda m: (m, 0)), pl.BlockSpec((n, d), lambda m: (0, 0)), row],
+        in_specs=[pl.BlockSpec((tm, n), lambda m: (m, 0)), pl.BlockSpec((None, n, d), lambda m: (layer, 0, 0)), row],
         out_specs=(row, row),
         compiler_params=params(1),
         cost_estimate=cost(2 * tokens * d * n, 2 * tokens * (3 * d + n)),
@@ -89,9 +289,9 @@
     )(p, wd, h)
 
 
-def inner(a, dy, wg, wu, wd, tm=512, tn=704):
+def inner(a, dy, wg, wu, wd, layer, tm=512, tn=704):
     tokens, d = a.shape
-    n = wd.shape[0]
+    n = wd.shape[1]
 
     def kernel(a, dy, g, u, w, o):
         gate, up = dot(whole(g), a[...], TB), dot(whole(u), a[...], TB)
@@ -102,13 +302,13 @@
         o[1] = (by_p * up * (sig * (1.0 + gate * (1.0 - sig)))).astype(BF)
         o[2] = (by_p * act).astype(BF)
 
-    w = pl.BlockSpec((4, tn, d // 4), lambda n, m: (0, n, 0))
+    w = pl.BlockSpec((None, 4, tn, d // 4), lambda n, m: (layer, 0, n, 0))
     act = pl.BlockSpec((tm, d), lambda n, m: (m, 0))
     return pl.pallas_call(
         kernel,
         out_shape=jax.ShapeDtypeStruct((3, n, tokens), BF),
         grid=(n // tn, tokens // tm),
-        in_specs=[act, act, w, w, pl.BlockSpec((tn, d), lambda n, m: (n, 0))],
+        in_specs=[act, act, w, w, pl.BlockSpec((None, tn, d), lambda n, m: (layer, n, 0))],
         out_specs=pl.BlockSpec((3, tn, tm), lambda n, m: (0, n, m)),
         compiler_params=params(2),
         cost_estimate=cost(6 * tokens * d * n, 2 * tokens * (2 * d + 3 * n)),
@@ -116,7 +316,7 @@
     )(a, dy, wg, wu, wd)
 
 
-def below(x, wg, wu, h, dh, tm=256):
+def below(x, wg, wu, layer, h, dh, tm=256):
     tokens, d = h.shape
     n = x.shape[1]
 
@@ -128,7 +328,7 @@
         o[...] = dh[...] + by_h.astype(BF)
 
     row = pl.BlockSpec((tm, d), lambda m: (m, 0))
-    w = pl.BlockSpec((4, n, d // 4), lambda m: (0, 0, 0))
+    w = pl.BlockSpec((None, 4, n, d // 4), lambda m: (layer, 0, 0, 0))
 
     def two(x_gate, x_up, g, u, h, dh, o):
         kernel((x_gate[0], x_up[0]), g, u, h, dh, o)
@@ -160,8 +360,8 @@
     slots = 4
 
     def kernel(*refs):
-        x_refs, r_refs = refs[:layers], refs[layers : 3 * layers]
-        out, right, acc, csend, crecv, mine, xsend, xrecv, ysend, yrecv, zsend, zrecv, rsem, csems, xsems, ysems, zsems = refs[3 * layers :]
+        x_refs, r_refs = refs[: 2 * layers], refs[2 * layers : 4 * layers]
+        out, right, acc, csend, crecv, mine, xsend, xrecv, ysend, yrecv, zsend, zrecv, rsem, csems, xsems, ysems, zsems = refs[4 * layers :]
         t = pl.program_id(0)
         s, r = lax.axis_index("s"), lax.axis_index("r")
         core, x, y, z = s % 2, s // 2, r // 2, r % 2
@@ -214,13 +414,13 @@
 
             @pl.when((t >= first) & (t < first + per))
             def _():
-                o = dot(x_refs[layer][...].reshape(4 * ROWS, tokens), right[0], NN)
+                o = dot(x_refs[2 * layer][...].reshape(4 * ROWS, tokens), right[0], NN)
                 for q in range(4):
                     acc[t % 2, q] = o[ROWS * q : ROWS * (q + 1)]
 
             @pl.when((t >= first + per) & (t < first + 3 * per))
             def _():
-                o = dot(x_refs[layer][...].reshape(4 * ROWS, tokens), right[1], NN)
+                o = dot(x_refs[2 * layer + 1][...], right[1], NN)
                 for q in range(4):
                     for p in range(4):
                         acc[t % 2, p, :, wide * q : wide * (q + 1)] = o[ROWS * q : ROWS * (q + 1), wide * p : wide * (p + 1)]
@@ -260,11 +460,14 @@
             along_core(t).start()
 
     def lhs(layer):
-        def index(t):
-            u = jnp.clip(t - layer * 3 * per, 0, 3 * per - 1)
-            return u // per, 0, u % per, 0
-
-        return pl.BlockSpec((1, 4, ROWS, tokens), index)
+        def pieces(t):
+            return 0, 0, jnp.clip(t - layer * 3 * per, 0, per - 1), 0
+
+        def rows(t):
+            u = jnp.clip(t - layer * 3 * per - per, 0, 2 * per - 1)
+            return 1 + u // per, u % per, 0
+
+        return [pl.BlockSpec((None, 4, ROWS, tokens), pieces), pl.BlockSpec((None, 4 * ROWS, tokens), rows)]
 
     block = (ROWS, d)
     dma = pltpu.SemaphoreType.DMA
@@ -272,7 +475,7 @@
         kernel,
         out_shape=jax.ShapeDtypeStruct((chunks,) + block, BF),
         grid=(chunks + LAG[4],),
-        in_specs=[lhs(layer) for layer in range(layers)] + [pl.BlockSpec(memory_space=pl.ANY)] * (2 * layers),
+        in_specs=[spec for layer in range(layers) for spec in lhs(layer)] + [pl.BlockSpec(memory_space=pl.ANY)] * (2 * layers),
         out_specs=pl.BlockSpec((1,) + block, lambda t: (jnp.maximum(t - LAG[4], 0), 0, 0)),
         scratch_shapes=[
             pltpu.VMEM((2, tokens, d), BF),
@@ -286,47 +489,59 @@
         compiler_params=params(1, collective_id=0, has_side_effects=True),
         cost_estimate=cost(2 * chunks * 4 * ROWS * tokens * d, 2 * layers * tokens * (3 * n + 2 * d)),
         name="summed",
-    )(*[x.reshape(3, 4, quarter, tokens) for x in xs], *[r for pair in rights for r in pair])
+    )(*[view for x in xs for view in (x.reshape(3, 4, quarter, tokens), x)], *[r for pair in rights for r in pair])
+
+
+def stepped(g, weights, ms, vs):
+    layers, quarter, d = weights[2].shape
+    per = quarter // ROWS
+    wide = d // 4
+
+    def kernel(*refs):
+        for j in range(3):
+            g = refs[j][...].astype(F32)
+            if j < 2:
+                g = jnp.concatenate([g[:, wide * q : wide * (q + 1)] for q in range(4)], axis=0).T
+            new = adamw(refs[3 + j][...].astype(F32), refs[6 + j][...], refs[9 + j][...], g)
+            for which in range(3):
+                refs[12 + 3 * which + j][...] = new[which]
+
+    def chunk(j):
+        return pl.BlockSpec((None, ROWS, d), lambda l, k: ((layers - 1 - l) * 3 * per + j * per + k, 0, 0))
+
+    column = pl.BlockSpec((None, wide, 4 * ROWS), lambda l, k: (l, 0, k))
+    blocks = [column, column, pl.BlockSpec((None, ROWS, d), lambda l, k: (l, k, 0))]
+    return pl.pallas_call(
+        kernel,
+        out_shape=tuple(jax.ShapeDtypeStruct(a.shape, a.dtype) for a in (*weights, *ms, *vs)),
+        grid=(layers, per),
+        in_specs=[chunk(1), chunk(2), chunk(0)] + blocks * 3,
+        out_specs=tuple(blocks * 3),
+        compiler_params=params(2),
+        cost_estimate=cost(20 * layers * 3 * quarter * d, 22 * layers * 3 * quarter * d),
+        name="stepped",
+    )(g, g, g, *weights, *ms, *vs)
 
 
 def solution(mesh):
     def step(x, dy, *arrays):
         weights, m, v = (arrays[i : i + 3] for i in (0, 3, 6))
-        layers = weights[0].shape[0]
-
-        def fetched(number):
-            gate, up = (lax.all_gather(w[number].T, "s", axis=0) for w in weights[:2])
-            return gate, up, lax.all_gather(weights[2][number], "s", axis=0, tiled=True)
-
-        full = [fetched(number) for number in range(layers)]
-        h, kept = x[0], []
-        a = normed(h)
-        for number in range(layers):
-            kept.append((h, a))
-            if number + 1 < layers:
-                gate, up, wd = full[number]
-                h, a = down(hidden(a, gate, up), wd, h)
+        layers, quarter, d = weights[2].shape
+        h = x[0]
+        p, a, gate, up, wd = started(h, *weights)
+        wd = wd.reshape(layers, 4 * quarter, d)
+        kept = [(h, a)]
+        h, a = down(p, wd, 0, h)
+        kept.append((h, a))
         by_h = dy[0]
         xs, rights = [], []
         for number in reversed(range(layers)):
-            gate, up, wd = full[number]
             h, a = kept[number]
-            xs.append(inner(a, by_h, gate, up, wd))
+            xs.append(inner(a, by_h, gate, up, wd, number))
             rights.append((by_h, a))
             if number:
-                by_h = below(xs[-1], gate, up, h, by_h)
-        g = summed(xs, rights)
-        g = g.reshape(layers, 3, -1, ROWS, g.shape[-1])[::-1]
-        quarter = g.shape[2] * ROWS
-        by_down = g[:, 0].reshape(layers, quarter, -1)
-
-        def turned(g):
-            g = g.reshape(layers, -1, ROWS, 4, g.shape[-1] // 4)
-            return g.transpose(0, 4, 3, 1, 2).reshape(layers, g.shape[-1], 4 * quarter)
-
-        gradients = [turned(g[:, 1]), turned(g[:, 2]), by_down]
-        new = [adamw(w.astype(F32), m, v, g.astype(F32)) for w, m, v, g in zip(weights, m, v, gradients, strict=True)]
-        return tuple(one[which] for which in range(3) for one in new)
+                by_h = below(xs[-1], gate, up, number, h, by_h)
+        return stepped(summed(xs, rights), weights, m, v)
 
     states, cut = P(("rep", "r", "s"), None, None), P(None, "s", None)
     return jax.shard_map(

time: 868 us -> 641 us (0.74); the launches traced: 857 us -> 641 us
  local copies, waits for them, and re-layouts: 140 us -> 0 us
  waiting for transfers between devices: 99.4 us -> 0 us
  Pallas kernels: 557 us -> 640 us
  other arithmetic: 46.5 us -> 0 us
  between operations: 14.7 us -> 0.82 us
    all_gather x6 -> x0, waiting for transfers between devices: 97.6 us -> none  [the longest x4 97.6 us: fetched(): gate, up = (lax.all_gather(w[number].T, 's', axis=0) for w in weights[:2])]
    pallas_call x1 -> x2, Pallas kernels: 60.3 us -> 143 us  [the longest x1 106 us: started(): pl.pallas_call(kernel, out_shape=(jax.ShapeDtypeStruct((tokens, n), BF),...]
    unnamed x30 -> x0, local copies, waits for them, and re-layouts: 66.6 us -> none
    convert_element_type x5 -> x0, other arithmetic: 41.4 us -> none  [the longest x3 27.6 us: adamw(): return ((w - 0.02 * step).astype(BF), m, v)]
    all_gather x4 -> x0, local copies, waits for them, and re-layouts: 33.2 us -> none  [fetched(): gate, up = (lax.all_gather(w[number].T, 's', axis=0) for w in weights[:2])]
    convert_element_type x4 -> x0, local copies, waits for them, and re-layouts: 23.6 us -> none  [step(): g.astype(F32)]
    slice x3 -> x0, local copies, waits for them, and re-layouts: 10.7 us -> none  [the longest x2 7.11 us: step(): by_down = g[:, 0].reshape(layers, quarter, -1)]
  transfers between devices with their start and end apart: 6 -> 0, of which waited for: 3 -> 0; matrix products, arithmetic and copies ran while one was open for 10% -> 0% of each run, Pallas kernels for 11% -> 0%
where the time goes in v2:
time: 641 us
  Pallas kernels  640 us (100%)
    pallas_call x1, Pallas kernels, summed(): pl.pallas_call(kernel, out_shape=jax.ShapeDtypeStruct((chunks,) + block,...  212 us
    pallas_call x2, Pallas kernels, inner(): pl.pallas_call(kernel, out_shape=jax.ShapeDtypeStruct((3, n, tokens), BF)...  192 us
    pallas_call x1, Pallas kernels, started(): pl.pallas_call(kernel, out_shape=(jax.ShapeDtypeStruct((tokens, n), BF),...  106 us
    pallas_call x1, Pallas kernels, below(): pl.pallas_call(two, out_shape=jax.ShapeDtypeStruct((tokens, d), BF), grid...  61.7 us
    pallas_call x1, Pallas kernels, stepped(): pl.pallas_call(kernel, out_shape=tuple((jax.ShapeDtypeStruct(a.shape, a.d...  36.1 us
    pallas_call x1, Pallas kernels, down(): pl.pallas_call(kernel, out_shape=(jax.ShapeDtypeStruct((tokens, d), BF),)...  32.4 us

profile of v2, /device:TPU:0, one launch (start us, length us, event | category | flops | bytes accessed | tf_op | source)
XLA Modules:
  0.0 640.6 jit_solution(14197659748840072058)
XLA Ops:
  0.6 106.4 %started.1 = (bf16[4096,2816]{1,0:T(8,128)(2,1)}, bf16[4096,1024]{1,0:T(8,128)(2,1)}, bf16[2,4,2816,256]{3,2,1,0:T(8,128)(2,1)}, bf16[2,4,2816,256]{3,2,1,0:T(8,128)(2,1)}, bf16[2,4,704,1024]{3,2,1,0:T(8,128)(2,1)}) custom-call(bf16[4096,1024]{1,0:T(8,128)(2,1)} %bitcast.8, bf16[2,256,2816]{2,1,0:T(8,128)(2,1)} %refs_3_.1, bf16[2,256,2816]{2,1,0:T(8,128)(2,1)} %refs_4_.1, ...), custom_call_target="tpu_custom_call" | custom-call | flops 47244640256 | bytes 31457280 | tf_op jit(solution)/shard_map/started/pallas_call | solution.py:242
  107.1 32.4 %down.1 = (bf16[4096,1024]{1,0:T(8,128)(2,1)}, bf16[4096,1024]{1,0:T(8,128)(2,1)}) custom-call(bf16[4096,2816]{1,0:T(8,128)(2,1)} %get-tuple-element.16.p, bf16[2,2816,1024]{2,1,0:T(8,128)(2,1)} %bitcast.10, bf16[4096,1024]{1,0:T(8,128)(2,1)} %bitcast.9), custom_call_target="tpu_custom_call" | custom-call | flops 23622320128 | bytes 48234496 | tf_op jit(solution)/shard_map/down/pallas_call | solution.py:280
  139.5 95.6 %inner.2.x_gate.x_up.refs_1_ = bf16[3,2816,4096]{2,1,0:T(8,128)(2,1)} custom-call(bf16[4096,1024]{1,0:T(8,128)(2,1)} %get-tuple-element.18.a.refs_5_, bf16[4096,1024]{1,0:T(8,128)(2,1)} %bitcast.5, bf16[2,4,2816,256]{3,2,1,0:T(8,128)(2,1)} %get-tuple-element.19.g, bf16[2,4,2816,256]{3,2,1,0:T(8,128)(2,1)} %get-tuple-element.20.u, bf16[2,2816,1024]{2,1,0:T(8,128)(2,1)} %bitcast.11), custom_call_target="tpu_custom_call" | custom-call | flops 70866960384 | bytes 85983232 | tf_op jit(solution)/shard_map/inner/pallas_call | solution.py:307
  235.2 61.7 %below.1.dy.refs_6_ = bf16[4096,1024]{1,0:T(8,128)(2,1)} custom-call(bf16[3,2816,4096]{2,1,0:T(8,128)(2,1)} %inner.2.x_gate.x_up.refs_1_, bf16[3,2816,4096]{2,1,0:T(8,128)(2,1)} %inner.2.x_gate.x_up.refs_1_, bf16[2,4,2816,256]{3,2,1,0:T(8,128)(2,1)} %get-tuple-element.19.g, bf16[2,4,2816,256]{3,2,1,0:T(8,128)(2,1)} %get-tuple-element.20.u, ...), custom_call_target="tpu_custom_call" | custom-call | flops 47244640256 | bytes 71303168 | tf_op jit(solution)/shard_map/below/pallas_call | solution.py:336
  296.9 95.9 %inner.3.refs_3_ = bf16[3,2816,4096]{2,1,0:T(8,128)(2,1)} custom-call(bf16[4096,1024]{1,0:T(8,128)(2,1)} %get-tuple-element.21.a.refs_7_, bf16[4096,1024]{1,0:T(8,128)(2,1)} %below.1.dy.refs_6_, bf16[2,4,2816,256]{3,2,1,0:T(8,128)(2,1)} %get-tuple-element.19.g, bf16[2,4,2816,256]{3,2,1,0:T(8,128)(2,1)} %get-tuple-element.20.u, bf16[2,2816,1024]{2,1,0:T(8,128)(2,1)} %bitcast.12), custom_call_target="tpu_custom_call" | custom-call | flops 70866960384 | bytes 85983232 | tf_op jit(solution)/shard_map/inner/pallas_call | solution.py:307
  392.8 211.6 %summed.1.refs_0_.refs_1_.refs_2_ = bf16[66,64,1024]{2,1,0:T(8,128)(2,1)} custom-call(bf16[3,4,704,4096]{3,2,1,0:T(8,128)(2,1)} %bitcast.3.refs_0_, bf16[3,2816,4096]{2,1,0:T(8,128)(2,1)} %inner.2.x_gate.x_up.refs_1_, bf16[3,4,704,4096]{3,2,1,0:T(8,128)(2,1)} %bitcast.4.refs_2_, bf16[3,2816,4096]{2,1,0:T(8,128)(2,1)} %inner.3.refs_3_, ...), custom_call_target="tpu_custom_call" | custom-call | flops 141733920768 | bytes 171966464 | tf_op jit(solution)/shard_map/summed/pallas_call | solution.py:474
  604.4 36.1 %stepped.1 = (bf16[2,256,2816]{2,1,0:T(8,128)(2,1)}, bf16[2,256,2816]{2,1,0:T(8,128)(2,1)}, bf16[2,704,1024]{2,1,0:T(8,128)(2,1)}, f32[2,256,2816]{2,1,0:T(8,128...) custom-call(bf16[66,64,1024]{2,1,0:T(8,128)(2,1)} %summed.1.refs_0_., ...), custom_call_target="tpu_custom_call" | custom-call | flops 86507520 | bytes 95158272 | tf_op jit(solution)/shard_map/stepped/pallas_call | solution.py:514

commit v3 on v2

--- a/solution.py
+++ b/solution.py
@@ -46,61 +46,89 @@
     return pl.CostEstimate(flops=flops, bytes_accessed=bytes_, transcendentals=0)
 
 
-def started(x, w_gate, w_up, w_down, tm=512, tn=1408):
+def routes(sems):
+    s, r = lax.axis_index("s"), lax.axis_index("r")
+    core, px, py, pz = s % 2, s // 2, r // 2, r % 2
+    sx = s + 2 - 4 * px
+    to_core, to_x = {"s": s + 1 - 2 * core}, {"s": sx}
+    to_y, to_z = {"r": r + 2 - 4 * py}, {"r": r + 1 - 2 * pz}
+
+    def item(number, own, full, base, size, by):
+        def copy(kind, src, dst, to):
+            return pltpu.make_async_remote_copy(
+                src_ref=src, dst_ref=dst, send_sem=sems.at[0, number, kind], recv_sem=sems.at[1, number, kind],
+                device_id=to, device_id_type=MESH,
+            )
+
+        def relay(kind, rows, to):
+            return copy(kind, full(sx, rows), full(sx, rows), to)
+
+        every = pl.ds(base, size)
+        if by in ("y", "z"):
+            half = size // 2
+            par = py if by == "y" else pz
+            mine, theirs = pl.ds(base + par * half, half), pl.ds(base + (1 - par) * half, half)
+            out = {
+                "x": copy(0, own(mine), full(s, mine), to_x),
+                "r": relay(2, mine, to_y if by == "y" else to_z),
+                "cx": relay(3, mine, to_core),
+                "cr": relay(4, theirs, to_core),
+            }
+        else:
+            part = size // 4
+
+            def at(y, z):
+                return pl.ds(base + (2 * y + z) * part, part)
+
+            mine = at(py, pz)
+            out = {
+                "x": copy(0, own(mine), full(s, mine), to_x),
+                "y": relay(2, mine, to_y),
+                "z": relay(3, mine, to_z),
+                "cx": relay(4, mine, to_core),
+                "cy": relay(5, at(1 - py, pz), to_core),
+                "cz": relay(6, at(py, 1 - pz), to_core),
+                "d": relay(7, at(1 - py, pz), to_z) if by == "yz" else relay(7, at(py, 1 - pz), to_y),
+                "cd": relay(8, at(1 - py, 1 - pz), to_core),
+            }
+        out["c"] = copy(1, own(every), full(s, every), to_core)
+        return out
+
+    return item, s, (to_core, to_x, to_y, to_z)
+
+
+def greet(partners):
+    barrier = pltpu.get_barrier_semaphore()
+    for to in partners:
+        pl.semaphore_signal(barrier, inc=1, device_id=to, device_id_type=MESH)
+    pl.semaphore_wait(barrier, len(partners))
+
+
+def got(one, *kinds):
+    for kind in kinds:
+        one[kind].wait_recv()
+
+
+def go(one, *kinds):
+    for kind in kinds:
+        one[kind].start()
+
+
+FOUR = ("c", "cx", "cy", "cz", "cd")
+TILES = (512, 896, 1408)
+
+
+def started(x, w_gate, w_up, w_down, tm=512):
     tokens, d = x.shape
     layers, wide, n = w_gate.shape
     quarter = n // 4
     steps_m = tokens // tm
-    last = (n // tn) * steps_m
-
-    def kernel(x_ref, g_ref, u_ref, d_ref, p_ref, a_ref, fg, fu, fd, a, g0, u0, turned, flat, dv, sems, local):
-        t = pl.program_id(0) * steps_m + pl.program_id(1)
-        s, r = lax.axis_index("s"), lax.axis_index("r")
-        core, px, py, pz = s % 2, s // 2, r // 2, r % 2
-        sx = s + 2 - 4 * px
-        to_core, to_x = {"s": s + 1 - 2 * core}, {"s": sx}
-        to_y, to_z = {"r": r + 2 - 4 * py}, {"r": r + 1 - 2 * pz}
-
-        def item(number, own, full, base, size, by):
-            def copy(kind, src, dst, to):
-                return pltpu.make_async_remote_copy(
-                    src_ref=src, dst_ref=dst, send_sem=sems.at[0, number, kind], recv_sem=sems.at[1, number, kind],
-                    device_id=to, device_id_type=MESH,
-                )
-
-            def relay(kind, rows, to):
-                return copy(kind, full(sx, rows), full(sx, rows), to)
-
-            every = pl.ds(base, size)
-            if by in ("y", "z"):
-                half = size // 2
-                par = py if by == "y" else pz
-                mine, theirs = pl.ds(base + par * half, half), pl.ds(base + (1 - par) * half, half)
-                out = {
-                    "x": copy(0, own(mine), full(s, mine), to_x),
-                    "r": relay(2, mine, to_y if by == "y" else to_z),
-                    "cx": relay(3, mine, to_core),
-                    "cr": relay(4, theirs, to_core),
-                }
-            else:
-                part = size // 4
-
-                def at(y, z):
-                    return pl.ds(base + (2 * y + z) * part, part)
-
-                mine = at(py, pz)
-                out = {
-                    "x": copy(0, own(mine), full(s, mine), to_x),
-                    "y": relay(2, mine, to_y),
-                    "z": relay(3, mine, to_z),
-                    "cx": relay(4, mine, to_core),
-                    "cy": relay(5, at(1 - py, pz), to_core),
-                    "cz": relay(6, at(py, 1 - pz), to_core),
-                    "d": relay(7, at(1 - py, pz), to_z) if by == "yz" else relay(7, at(py, 1 - pz), to_y),
-                    "cd": relay(8, at(1 - py, 1 - pz), to_core),
-                }
-            out["c"] = copy(1, own(every), full(s, every), to_core)
-            return out
+    bases = tuple(sum(TILES[:i]) for i in range(len(TILES)))
+    last = len(TILES) * steps_m
+
+    def kernel(x_ref, g_ref, u_ref, d_ref, p0, p1, p2, a_ref, fg, fu, fd, a, g0, u0, turned, flat, dv, sems, local):
+        t = pl.program_id(0)
+        item, s, partners = routes(sems)
 
         def inside(ref):
             return (lambda rows: ref.at[s, rows]), (lambda block, rows: ref.at[block, rows])
@@ -108,56 +136,42 @@
         def outside(own, ref):
             return (lambda rows: own.at[rows]), (lambda block, rows: ref.at[1, block, rows])
 
-        g0a, u0a = item(0, *inside(g0), 0, tn, "y"), item(1, *inside(u0), 0, tn, "z")
-        g0b, u0b = item(2, *inside(g0), tn, tn, "y"), item(3, *inside(u0), tn, tn, "z")
-        d0 = item(4, lambda rows: d_ref.at[0, rows], lambda block, rows: fd.at[0, block, rows], 0, quarter, "yz")
-        g1 = item(5, *outside(turned.at[0], fg), 0, n, "zy")
-        u1 = item(6, *outside(turned.at[1], fu), 0, n, "yz")
-        d1 = item(7, lambda rows: d_ref.at[1, rows], lambda block, rows: fd.at[1, block, rows], 0, quarter, "zy")
-        items = (g0a, u0a, g0b, u0b, d0, g1, u1, d1)
+        tiles = [
+            (item(2 * i, *inside(g0), bases[i], TILES[i], "y"), item(2 * i + 1, *inside(u0), bases[i], TILES[i], "z"))
+            for i in range(len(TILES))
+        ]
+        d0 = item(6, lambda rows: d_ref.at[0, rows], lambda block, rows: fd.at[block, rows], 0, quarter, "yz")
+        half = n // 2
+        g1a, u1a = item(7, *outside(turned.at[0], fg), 0, half, "zy"), item(8, *outside(turned.at[1], fu), 0, half, "yz")
+        g1b, u1b = item(9, *outside(turned.at[0], fg), half, half, "zy"), item(10, *outside(turned.at[1], fu), half, half, "yz")
+        late = (d0, g1a, u1a, g1b, u1b)
 
         def here(k, src, dst):
             return pltpu.make_async_copy(src, dst, local.at[k])
 
         loads = [here(2 * i + j, ref.at[i], flat.at[2 * i + j]) for i in range(2) for j, ref in enumerate((g_ref, u_ref))]
-        load_x, load_d = here(4, x_ref, a), here(5, d_ref, dv)
+        load_x, load_d = here(4, x_ref, a), here(5, d_ref.at[0], dv)
         keep = [
             here(6, turned.at[0], fg.at[1, s]),
             here(7, turned.at[1], fu.at[1, s]),
-            here(8, dv.at[0], fd.at[0, s]),
-            here(9, dv.at[1], fd.at[1, s]),
-            here(10, a, a_ref),
-            here(11, g0, fg.at[0]),
-            here(12, u0, fu.at[0]),
+            here(8, dv, fd.at[s]),
+            here(9, a, a_ref),
+            here(10, g0, fg.at[0]),
+            here(11, u0, fu.at[0]),
         ]
-
-        def begin(one):
-            one["x"].start()
-            one["c"].start()
-
-        def got(one, *kinds):
-            for kind in kinds:
-                one[kind].wait_recv()
-
-        def go(one, *kinds):
-            for kind in kinds:
-                one[kind].start()
 
         @pl.when(t == 0)
         def _():
             for load in (*loads[:2], load_x, load_d, *loads[2:]):
                 load.start()
-            barrier = pltpu.get_barrier_semaphore()
-            for to in (to_core, to_x, to_y, to_z):
-                pl.semaphore_signal(barrier, inc=1, device_id=to, device_id_type=MESH)
-            pl.semaphore_wait(barrier, 4)
+            greet(partners)
             loads[0].wait()
             loads[1].wait()
-            for base, pair in ((0, (g0a, u0a)), (tn, (g0b, u0b))):
+            for base, size, pair in zip(bases, TILES, tiles, strict=True):
                 for j, (ref, one) in enumerate(zip((g0, u0), pair, strict=True)):
-                    ref[s, base : base + tn] = flat[j, :, base : base + tn].T
-                    begin(one)
-            begin(d0)
+                    ref[s, base : base + size] = flat[j, :, base : base + size].T
+                    go(one, "x", "c")
+            go(d0, "x", "c")
             load_x.wait()
 
             @pl.loop(0, steps_m)
@@ -165,27 +179,25 @@
                 rows = pl.ds(i * tm, tm)
                 a[rows, :] = normed(a[rows, :])
 
-            keep[4].start()
-            got(g0a, "x")
-            go(g0a, "r", "cx")
-            for j, one in enumerate((g1, u1)):
+            keep[3].start()
+            g00, u00 = tiles[0]
+            got(g00, "x")
+            go(g00, "r", "cx")
+            got(u00, "x")
+            go(u00, "r", "cx")
+            got(g00, "r")
+            go(g00, "cr")
+            got(u00, "r")
+            go(u00, "cr")
+            for j in range(2):
                 loads[2 + j].wait()
-                for base in (0, tn):
-                    turned[j, base : base + tn] = flat[2 + j, :, base : base + tn].T
-                begin(one)
+                for base in (0, half):
+                    turned[j, base : base + half] = flat[2 + j, :, base : base + half].T
                 keep[j].start()
-            begin(d1)
+            for one in late[1:]:
+                go(one, "x", "c")
             load_d.wait()
             keep[2].start()
-            keep[3].start()
-            got(u0a, "x")
-            go(u0a, "r", "cx")
-            got(g0a, "r")
-            go(g0a, "cr")
-            got(u0a, "r")
-            go(u0a, "cr")
-            got(g0a, "c", "cx", "cr")
-            got(u0a, "c", "cx", "cr")
 
         def on(step, *todo):
             @pl.when(t == step)
@@ -194,47 +206,57 @@
                     got(one, *wait)
                     go(one, *then)
 
-        on(1, (g0b, ("x",), ("r", "cx")))
-        on(3, (u0b, ("x",), ("r", "cx")))
-        on(4, (g0b, ("r",), ("cr",)))
-        on(5, (d0, ("x",), ("y", "z", "cx")))
-        on(6, (u0b, ("r",), ("cr",)))
-        on(7, (g1, ("x",), ("y", "z", "cx")))
-
-        @pl.when(t == steps_m)
-        def _():
-            got(g0b, "c", "cx", "cr")
-            got(u0b, "c", "cx", "cr")
-            keep[5].start()
-            keep[6].start()
-
-        on(8, (d0, ("y", "z"), ("cy", "cz", "d")))
-        on(9, (u1, ("x",), ("y", "z", "cx")))
-        on(10, (g1, ("y", "z"), ("cy", "cz", "d")))
-        on(11, (d1, ("x",), ("y", "z", "cx")), (d0, ("d",), ("cd",)))
-        on(12, (u1, ("y", "z"), ("cy", "cz", "d")))
-        on(13, (g1, ("d",), ("cd",)))
-        on(14, (d1, ("y", "z"), ("cy", "cz", "d")))
-        on(15, (u1, ("d",), ("cd",)))
-
-        rows = pl.ds(pl.program_id(1) * tm, tm)
-        columns = pl.ds(pl.program_id(0) * tn, tn)
-        block = a[rows, :]
-        gate = dot(block, whole([g0[q, columns] for q in range(4)]), TB)
-        up = dot(block, whole([u0[q, columns] for q in range(4)]), TB)
-        p_ref[...] = (gate * jax.nn.sigmoid(gate) * up).astype(BF)
+        (_, _), (g01, u01), (g02, u02) = tiles
+        first, second, third = (("x",), ("y", "z", "cx")), (("y", "z"), ("cy", "cz", "d")), (("d",), ("cd",))
+        near, far = (("x",), ("r", "cx")), (("r",), ("cr",))
+        on(1, (g01, *near))
+        on(3, (u01, *near))
+        on(6, (g01, *far))
+        on(8, (u01, *far), (g02, *near))
+        on(11, (u02, *near))
+        on(12, (g02, *far))
+        on(14, (d0, *first))
+        on(16, (u02, *far), (g1a, *first))
+        on(17, (u1a, *first))
+        on(18, (d0, *second), (g1b, *first))
+        on(19, (g1a, *second), (u1b, *first))
+        on(20, (u1a, *second))
+        on(21, (g1b, *second), (d0, *third))
+        on(22, (u1b, *second), (g1a, *third))
+        on(23, (u1a, *third))
+
+        for i, (base, size, pair, p_ref) in enumerate(zip(bases, TILES, tiles, (p0, p1, p2), strict=True)):
+
+            @pl.when(t == i * steps_m)
+            def _():
+                for one in pair:
+                    got(one, "c", "cx", "cr")
+                if i == len(TILES) - 1:
+                    keep[4].start()
+                    keep[5].start()
+
+            @pl.when((t >= i * steps_m) & (t < (i + 1) * steps_m))
+            def _():
+                block = a[pl.ds((t - i * steps_m) * tm, tm), :]
+                gate = dot(block, whole([g0[q, base : base + size] for q in range(4)]), TB)
+                up = dot(block, whole([u0[q, base : base + size] for q in range(4)]), TB)
+                p_ref[...] = (gate * jax.nn.sigmoid(gate) * up).astype(BF)
 
         @pl.when(t == last - 1)
         def _():
-            got(d1, "d")
-            go(d1, "cd")
-            for one in (d0, g1, u1, d1):
-                got(one, "c", "cx", "cy", "cz", "cd")
-            for one in items:
+            for one in (g1b, u1b):
+                got(one, "d")
+                go(one, "cd")
+            for one in late:
+                got(one, *FOUR)
+            for one in (*[one for pair in tiles for one in pair], *late):
                 for copy in one.values():
                     copy.wait_send()
             for copy in keep:
                 copy.wait()
+
+    def part(i):
+        return pl.BlockSpec((tm, TILES[i]), lambda t: (jnp.clip(t - i * steps_m, 0, steps_m - 1), 0))
 
     hbm = pl.BlockSpec(memory_space=pl.ANY)
     dma = pltpu.SemaphoreType.DMA
@@ -242,65 +264,117 @@
     return pl.pallas_call(
         kernel,
         out_shape=(
-            jax.ShapeDtypeStruct((tokens, n), BF),
+            *[jax.ShapeDtypeStruct((tokens, size), BF) for size in TILES],
             jax.ShapeDtypeStruct((tokens, d), BF),
             full,
             full,
-            jax.ShapeDtypeStruct((layers, 4, quarter, d), BF),
+            jax.ShapeDtypeStruct((4, quarter, d), BF),
         ),
-        grid=(n // tn, steps_m),
+        grid=(last,),
         in_specs=[hbm] * 4,
-        out_specs=(pl.BlockSpec((tm, tn), lambda n, m: (m, n)), hbm, hbm, hbm, hbm),
+        out_specs=(*[part(i) for i in range(len(TILES))], hbm, hbm, hbm, hbm),
         scratch_shapes=[
             pltpu.VMEM((tokens, d), BF),
             pltpu.VMEM((4, n, wide), BF),
             pltpu.VMEM((4, n, wide), BF),
             pltpu.VMEM((2, n, wide), BF),
             pltpu.VMEM((4, wide, n), BF),
-            pltpu.VMEM((layers, quarter, d), BF),
-            dma((2, 8, 9)),
-            dma((13,)),
+            pltpu.VMEM((quarter, d), BF),
+            dma((2, 11, 9)),
+            dma((12,)),
         ],
-        compiler_params=params(2, collective_id=1, has_side_effects=True),
+        compiler_params=params(1, collective_id=1, has_side_effects=True),
         cost_estimate=cost(4 * tokens * d * n, 2 * tokens * (d + n)),
         name="started",
     )(x, w_gate, w_up, w_down)
 
 
-def down(p, wd, layer, h, tm=512):
-    tokens, n = p.shape
-    d = h.shape[1]
-
-    def kernel(p, w, h, ho, ao):
-        new = h[...] + dot(p[...], w[...], NN).astype(BF)
+def down(ps, wd, h, w_down, tm=512):
+    tokens, d = h.shape
+    n = wd.shape[0]
+    quarter = n // 4
+    steps = tokens // tm
+    bases = tuple(sum(TILES[:i]) for i in range(len(TILES)))
+    cut = 384
+
+    def kernel(p0, p1, p2, w, h, d_ref, ho, ao, fd, dv, sems, local):
+        t = pl.program_id(0)
+        item, s, partners = routes(sems)
+
+        def one(number, base, size, by):
+            return item(number, lambda rows: d_ref.at[1, rows], lambda block, rows: fd.at[block, rows], base, size, by)
+
+        a, b = one(0, 0, cut, "yz"), one(1, cut, quarter - cut, "zy")
+        load = pltpu.make_async_copy(d_ref.at[1], dv, local.at[0])
+        keep = pltpu.make_async_copy(dv, fd.at[s], local.at[1])
+
+        @pl.when(t == 0)
+        def _():
+            load.start()
+            greet(partners)
+            for which in (a, b):
+                go(which, "x", "c")
+            load.wait()
+            keep.start()
+
+        for step, which, wait, then in (
+            (2, a, ("x",), ("y", "z", "cx")),
+            (3, b, ("x",), ("y", "z", "cx")),
+            (4, a, ("y", "z"), ("cy", "cz", "d")),
+            (5, b, ("y", "z"), ("cy", "cz", "d")),
+            (6, a, ("d",), ("cd",)),
+            (7, b, ("d",), ("cd",)),
+        ):
+
+            @pl.when(t == step)
+            def _():
+                got(which, *wait)
+                go(which, *then)
+
+        by_p = sum(dot(p[...], w[base : base + size], NN) for p, base, size in zip((p0, p1, p2), bases, TILES, strict=True))
+        new = h[...] + by_p.astype(BF)
         ho[...] = new
         ao[...] = normed(new)
 
+        @pl.when(t == steps - 1)
+        def _():
+            for which in (a, b):
+                got(which, *FOUR)
+                for copy in which.values():
+                    copy.wait_send()
+            keep.wait()
+
     row = pl.BlockSpec((tm, d), lambda m: (m, 0))
+    hbm = pl.BlockSpec(memory_space=pl.ANY)
+    dma = pltpu.SemaphoreType.DMA
     return pl.pallas_call(
         kernel,
-        out_shape=(jax.ShapeDtypeStruct((tokens, d), BF),) * 2,
-        grid=(tokens // tm,),
-        in_specs=[pl.BlockSpec((tm, n), lambda m: (m, 0)), pl.BlockSpec((None, n, d), lambda m: (layer, 0, 0)), row],
-        out_specs=(row, row),
-        compiler_params=params(1),
+        out_shape=(*[jax.ShapeDtypeStruct((tokens, d), BF)] * 2, jax.ShapeDtypeStruct((4, quarter, d), BF)),
+        grid=(steps,),
+        in_specs=[pl.BlockSpec((tm, size), lambda m: (m, 0)) for size in TILES] + [pl.BlockSpec((n, d), lambda m: (0, 0)), row, hbm],
+        out_specs=(row, row, hbm),
+        scratch_shapes=[pltpu.VMEM((quarter, d), BF), dma((2, 2, 9)), dma((2,))],
+        compiler_params=params(1, collective_id=2, has_side_effects=True),
         cost_estimate=cost(2 * tokens * d * n, 2 * tokens * (3 * d + n)),
         name="down",
-    )(p, wd, h)
-
-
-def inner(a, dy, wg, wu, wd, layer, tm=512, tn=704):
+    )(*ps, wd, h, w_down)
+
+
+def inner(a, dy, wg, wu, wd, layer, tm=1024, tn=704, lanes=256):
     tokens, d = a.shape
-    n = wd.shape[1]
+    n = wd.shape[0]
 
     def kernel(a, dy, g, u, w, o):
-        gate, up = dot(whole(g), a[...], TB), dot(whole(u), a[...], TB)
-        by_p = dot(w[...], dy[...], TB).astype(BF).astype(F32)
-        sig = jax.nn.sigmoid(gate)
-        act = gate * sig
-        o[0] = (act * up).astype(BF)
-        o[1] = (by_p * up * (sig * (1.0 + gate * (1.0 - sig)))).astype(BF)
-        o[2] = (by_p * act).astype(BF)
+        to_gate, to_up = whole(g), whole(u)
+        for start in range(0, tm, lanes):
+            part = slice(start, start + lanes)
+            gate, up = dot(to_gate, a[part], TB), dot(to_up, a[part], TB)
+            by_p = dot(w[...], dy[part], TB).astype(BF).astype(F32)
+            sig = 0.5 * jnp.tanh(0.5 * gate) + 0.5
+            act = gate * sig
+            o[0, :, part] = (act * up).astype(BF)
+            o[1, :, part] = (by_p * up * (sig * (1.0 + gate * (1.0 - sig)))).astype(BF)
+            o[2, :, part] = (by_p * act).astype(BF)
 
     w = pl.BlockSpec((None, 4, tn, d // 4), lambda n, m: (layer, 0, n, 0))
     act = pl.BlockSpec((tm, d), lambda n, m: (m, 0))
@@ -308,7 +382,7 @@
         kernel,
         out_shape=jax.ShapeDtypeStruct((3, n, tokens), BF),
         grid=(n // tn, tokens // tm),
-        in_specs=[act, act, w, w, pl.BlockSpec((None, tn, d), lambda n, m: (layer, n, 0))],
+        in_specs=[act, act, w, w, pl.BlockSpec((tn, d), lambda n, m: (n, 0))],
         out_specs=pl.BlockSpec((3, tn, tm), lambda n, m: (0, n, m)),
         compiler_params=params(2),
         cost_estimate=cost(6 * tokens * d * n, 2 * tokens * (2 * d + 3 * n)),
@@ -391,7 +465,6 @@
         @pl.when(t == 0)
         def _():
             load(0).start()
-            load(1).start()
             barrier = pltpu.get_barrier_semaphore()
             for to in ({"s": other}, {"s": over_x}, {"r": over_y}, {"r": over_z}):
                 pl.semaphore_signal(barrier, inc=1, device_id=to, device_id_type=MESH)
@@ -403,8 +476,7 @@
             @pl.when(t == first)
             def _():
                 load(2 * layer).wait()
-                if layer:
-                    load(2 * layer + 1).start()
+                load(2 * layer + 1).start()
 
             @pl.when(t == first + per)
             def _():
@@ -528,16 +600,15 @@
         weights, m, v = (arrays[i : i + 3] for i in (0, 3, 6))
         layers, quarter, d = weights[2].shape
         h = x[0]
-        p, a, gate, up, wd = started(h, *weights)
-        wd = wd.reshape(layers, 4 * quarter, d)
+        *ps, a, gate, up, wd0 = started(h, *weights)
         kept = [(h, a)]
-        h, a = down(p, wd, 0, h)
+        h, a, wd1 = down(ps, wd0.reshape(4 * quarter, d), h, weights[2])
         kept.append((h, a))
         by_h = dy[0]
         xs, rights = [], []
         for number in reversed(range(layers)):
             h, a = kept[number]
-            xs.append(inner(a, by_h, gate, up, wd, number))
+            xs.append(inner(a, by_h, gate, up, (wd0, wd1)[number].reshape(4 * quarter, d), number))
             rights.append((by_h, a))
             if number:
                 by_h = below(xs[-1], gate, up, number, h, by_h)

time: 641 us -> 617 us (0.963)
  Pallas kernels: 640 us -> 616 us
    pallas_call x2, Pallas kernels: 192 us -> 173 us  [inner(): pl.pallas_call(kernel, out_shape=jax.ShapeDtypeStruct((3, n, tokens), BF)...]
where the time goes in v3:
time: 617 us
  Pallas kernels  616 us (100%)
    pallas_call x1, Pallas kernels, summed(): pl.pallas_call(kernel, out_shape=jax.ShapeDtypeStruct((chunks,) + block,...  212 us
    pallas_call x2, Pallas kernels, inner(): pl.pallas_call(kernel, out_shape=jax.ShapeDtypeStruct((3, n, tokens), BF)...  173 us
    pallas_call x1, Pallas kernels, started(): pl.pallas_call(kernel, out_shape=(*[jax.ShapeDtypeStruct((tokens, size),...  95 us
    pallas_call x1, Pallas kernels, below(): pl.pallas_call(two, out_shape=jax.ShapeDtypeStruct((tokens, d), BF), grid...  61.7 us
    pallas_call x1, Pallas kernels, down(): pl.pallas_call(kernel, out_shape=(*[jax.ShapeDtypeStruct((tokens, d), BF)...  38 us
    pallas_call x1, Pallas kernels, stepped(): pl.pallas_call(kernel, out_shape=tuple((jax.ShapeDtypeStruct(a.shape, a.d...  36.1 us

profile of v3, /device:TPU:0, one launch (start us, length us, event | category | flops | bytes accessed | tf_op | source)
XLA Modules:
  0.0 616.9 jit_solution(2453435093263131159)
XLA Ops:
  0.6 95.0 %started.1 = (bf16[4096,512]{1,0:T(8,128)(2,1)}, bf16[4096,896]{1,0:T(8,128)(2,1)}, bf16[4096,1408]{1,0:T(8,128)(2,1)}, bf16[4096,1024]{1,0:T(8,128)(2,1)}, bf16...) custom-call(bf16[4096,1024]{1,0:T(8,128)(2,1)} %bitcast.9, ...), custom_call_target="tpu_custom_call" | custom-call | flops 47244640256 | bytes 31457280 | tf_op jit(solution)/shard_map/started/pallas_call | solution.py:264
  95.7 38.0 %down.1 = (bf16[4096,1024]{1,0:T(8,128)(2,1)}, bf16[4096,1024]{1,0:T(8,128)(2,1)}, bf16[4,704,1024]{2,1,0:T(8,128)(2,1)}) custom-call(bf16[4096,512]{1,0:T(8,128)(2,1)} %get-tuple-element.19.p0, bf16[4096,896]{1,0:T(8,128)(2,1)} %get-tuple-element.20.p1, bf16[4096,1408]{1,0:T(8,128)(2,1)} %get-tuple-element.21.p2, bf16[2816,1024]{1,0:T(8,128)(2,1)} %bitcast.11, ...), custom_call_target="tpu_custom_call" | custom-call | flops 23622320128 | bytes 48234496 | tf_op jit(solution)/shard_map/down/pallas_call | solution.py:350
  133.6 86.7 %inner.2.x_gate.x_up.refs_1_ = bf16[3,2816,4096]{2,1,0:T(8,128)(2,1)} custom-call(bf16[4096,1024]{1,0:T(8,128)(2,1)} %get-tuple-element.23.a.refs_5_, bf16[4096,1024]{1,0:T(8,128)(2,1)} %bitcast.6, bf16[2,4,2816,256]{3,2,1,0:T(8,128)(2,1)} %get-tuple-element.24.g, bf16[2,4,2816,256]{3,2,1,0:T(8,128)(2,1)} %get-tuple-element.25.u, bf16[2816,1024]{1,0:T(8,128)(2,1)} %bitcast.13), custom_call_target="tpu_custom_call" | custom-call | flops 70866960384 | bytes 85983232 | tf_op jit(solution)/shard_map/inner/pallas_call | solution.py:381
  220.3 61.7 %below.1.dy.refs_6_ = bf16[4096,1024]{1,0:T(8,128)(2,1)} custom-call(bf16[3,2816,4096]{2,1,0:T(8,128)(2,1)} %inner.2.x_gate.x_up.refs_1_, bf16[3,2816,4096]{2,1,0:T(8,128)(2,1)} %inner.2.x_gate.x_up.refs_1_, bf16[2,4,2816,256]{3,2,1,0:T(8,128)(2,1)} %get-tuple-element.24.g, bf16[2,4,2816,256]{3,2,1,0:T(8,128)(2,1)} %get-tuple-element.25.u, ...), custom_call_target="tpu_custom_call" | custom-call | flops 47244640256 | bytes 71303168 | tf_op jit(solution)/shard_map/below/pallas_call | solution.py:410
  282.0 86.5 %inner.3.refs_3_ = bf16[3,2816,4096]{2,1,0:T(8,128)(2,1)} custom-call(bf16[4096,1024]{1,0:T(8,128)(2,1)} %get-tuple-element.27.a.refs_7_, bf16[4096,1024]{1,0:T(8,128)(2,1)} %below.1.dy.refs_6_, bf16[2,4,2816,256]{3,2,1,0:T(8,128)(2,1)} %get-tuple-element.24.g, bf16[2,4,2816,256]{3,2,1,0:T(8,128)(2,1)} %get-tuple-element.25.u, bf16[2816,1024]{1,0:T(8,128)(2,1)} %bitcast.12), custom_call_target="tpu_custom_call" | custom-call | flops 70866960384 | bytes 85983232 | tf_op jit(solution)/shard_map/inner/pallas_call | solution.py:381
  368.5 212.1 %summed.1.refs_0_.refs_1_.refs_2_ = bf16[66,64,1024]{2,1,0:T(8,128)(2,1)} custom-call(bf16[3,4,704,4096]{3,2,1,0:T(8,128)(2,1)} %bitcast.4.refs_0_, bf16[3,2816,4096]{2,1,0:T(8,128)(2,1)} %inner.2.x_gate.x_up.refs_1_, bf16[3,4,704,4096]{3,2,1,0:T(8,128)(2,1)} %bitcast.5.refs_2_, bf16[3,2816,4096]{2,1,0:T(8,128)(2,1)} %inner.3.refs_3_, ...), custom_call_target="tpu_custom_call" | custom-call | flops 141733920768 | bytes 171966464 | tf_op jit(solution)/shard_map/summed/pallas_call | solution.py:546
  580.6 36.1 %stepped.1 = (bf16[2,256,2816]{2,1,0:T(8,128)(2,1)}, bf16[2,256,2816]{2,1,0:T(8,128)(2,1)}, bf16[2,704,1024]{2,1,0:T(8,128)(2,1)}, f32[2,256,2816]{2,1,0:T(8,128...) custom-call(bf16[66,64,1024]{2,1,0:T(8,128)(2,1)} %summed.1.refs_0_., ...), custom_call_target="tpu_custom_call" | custom-call | flops 86507520 | bytes 95158272 | tf_op jit(solution)/shard_map/stepped/pallas_call | solution.py:586

commit v4 on v3

--- a/solution.py
+++ b/solution.py
@@ -294,7 +294,6 @@
     n = wd.shape[0]
     quarter = n // 4
     steps = tokens // tm
-    bases = tuple(sum(TILES[:i]) for i in range(len(TILES)))
     cut = 384
 
     def kernel(p0, p1, p2, w, h, d_ref, ho, ao, fd, dv, sems, local):
@@ -331,7 +330,7 @@
                 got(which, *wait)
                 go(which, *then)
 
-        by_p = sum(dot(p[...], w[base : base + size], NN) for p, base, size in zip((p0, p1, p2), bases, TILES, strict=True))
+        by_p = dot(jnp.concatenate([p0[...], p1[...], p2[...]], axis=1), w[...], NN)
         new = h[...] + by_p.astype(BF)
         ho[...] = new
         ao[...] = normed(new)

time: 617 us -> 615 us (level)
  no operation moved by 1% of the time
where the time goes in v4:
time: 615 us
  Pallas kernels  614 us (100%)
    pallas_call x1, Pallas kernels, summed(): pl.pallas_call(kernel, out_shape=jax.ShapeDtypeStruct((chunks,) + block,...  212 us
    pallas_call x2, Pallas kernels, inner(): pl.pallas_call(kernel, out_shape=jax.ShapeDtypeStruct((3, n, tokens), BF)...  173 us
    pallas_call x1, Pallas kernels, started(): pl.pallas_call(kernel, out_shape=(*[jax.ShapeDtypeStruct((tokens, size),...  95 us
    pallas_call x1, Pallas kernels, below(): pl.pallas_call(two, out_shape=jax.ShapeDtypeStruct((tokens, d), BF), grid...  61.7 us
    pallas_call x1, Pallas kernels, down(): pl.pallas_call(kernel, out_shape=(*[jax.ShapeDtypeStruct((tokens, d), BF)...  36.2 us
    pallas_call x1, Pallas kernels, stepped(): pl.pallas_call(kernel, out_shape=tuple((jax.ShapeDtypeStruct(a.shape, a.d...  36.1 us

profile of v4, /device:TPU:0, one launch (start us, length us, event | category | flops | bytes accessed | tf_op | source)
XLA Modules:
  0.0 614.8 jit_solution(11789152404523771408)
XLA Ops:
  0.6 95.0 %started.1 = (bf16[4096,512]{1,0:T(8,128)(2,1)}, bf16[4096,896]{1,0:T(8,128)(2,1)}, bf16[4096,1408]{1,0:T(8,128)(2,1)}, bf16[4096,1024]{1,0:T(8,128)(2,1)}, bf16...) custom-call(bf16[4096,1024]{1,0:T(8,128)(2,1)} %bitcast.9, ...), custom_call_target="tpu_custom_call" | custom-call | flops 47244640256 | bytes 31457280 | tf_op jit(solution)/shard_map/started/pallas_call | solution.py:264
  95.7 36.2 %down.1 = (bf16[4096,1024]{1,0:T(8,128)(2,1)}, bf16[4096,1024]{1,0:T(8,128)(2,1)}, bf16[4,704,1024]{2,1,0:T(8,128)(2,1)}) custom-call(bf16[4096,512]{1,0:T(8,128)(2,1)} %get-tuple-element.19.p0, bf16[4096,896]{1,0:T(8,128)(2,1)} %get-tuple-element.20.p1, bf16[4096,1408]{1,0:T(8,128)(2,1)} %get-tuple-element.21.p2, bf16[2816,1024]{1,0:T(8,128)(2,1)} %bitcast.11, ...), custom_call_target="tpu_custom_call" | custom-call | flops 23622320128 | bytes 48234496 | tf_op jit(solution)/shard_map/down/pallas_call | solution.py:349
  131.9 86.7 %inner.2.x_gate.x_up.refs_1_ = bf16[3,2816,4096]{2,1,0:T(8,128)(2,1)} custom-call(bf16[4096,1024]{1,0:T(8,128)(2,1)} %get-tuple-element.23.a.refs_5_, bf16[4096,1024]{1,0:T(8,128)(2,1)} %bitcast.6, bf16[2,4,2816,256]{3,2,1,0:T(8,128)(2,1)} %get-tuple-element.24.g, bf16[2,4,2816,256]{3,2,1,0:T(8,128)(2,1)} %get-tuple-element.25.u, bf16[2816,1024]{1,0:T(8,128)(2,1)} %bitcast.13), custom_call_target="tpu_custom_call" | custom-call | flops 70866960384 | bytes 85983232 | tf_op jit(solution)/shard_map/inner/pallas_call | solution.py:380
  218.6 61.7 %below.1.dy.refs_6_ = bf16[4096,1024]{1,0:T(8,128)(2,1)} custom-call(bf16[3,2816,4096]{2,1,0:T(8,128)(2,1)} %inner.2.x_gate.x_up.refs_1_, bf16[3,2816,4096]{2,1,0:T(8,128)(2,1)} %inner.2.x_gate.x_up.refs_1_, bf16[2,4,2816,256]{3,2,1,0:T(8,128)(2,1)} %get-tuple-element.24.g, bf16[2,4,2816,256]{3,2,1,0:T(8,128)(2,1)} %get-tuple-element.25.u, ...), custom_call_target="tpu_custom_call" | custom-call | flops 47244640256 | bytes 71303168 | tf_op jit(solution)/shard_map/below/pallas_call | solution.py:409
  280.3 86.5 %inner.3.refs_3_ = bf16[3,2816,4096]{2,1,0:T(8,128)(2,1)} custom-call(bf16[4096,1024]{1,0:T(8,128)(2,1)} %get-tuple-element.27.a.refs_7_, bf16[4096,1024]{1,0:T(8,128)(2,1)} %below.1.dy.refs_6_, bf16[2,4,2816,256]{3,2,1,0:T(8,128)(2,1)} %get-tuple-element.24.g, bf16[2,4,2816,256]{3,2,1,0:T(8,128)(2,1)} %get-tuple-element.25.u, bf16[2816,1024]{1,0:T(8,128)(2,1)} %bitcast.12), custom_call_target="tpu_custom_call" | custom-call | flops 70866960384 | bytes 85983232 | tf_op jit(solution)/shard_map/inner/pallas_call | solution.py:380
  366.8 211.7 %summed.1.refs_0_.refs_1_.refs_2_ = bf16[66,64,1024]{2,1,0:T(8,128)(2,1)} custom-call(bf16[3,4,704,4096]{3,2,1,0:T(8,128)(2,1)} %bitcast.4.refs_0_, bf16[3,2816,4096]{2,1,0:T(8,128)(2,1)} %inner.2.x_gate.x_up.refs_1_, bf16[3,4,704,4096]{3,2,1,0:T(8,128)(2,1)} %bitcast.5.refs_2_, bf16[3,2816,4096]{2,1,0:T(8,128)(2,1)} %inner.3.refs_3_, ...), custom_call_target="tpu_custom_call" | custom-call | flops 141733920768 | bytes 171966464 | tf_op jit(solution)/shard_map/summed/pallas_call | solution.py:545
  578.5 36.1 %stepped.1 = (bf16[2,256,2816]{2,1,0:T(8,128)(2,1)}, bf16[2,256,2816]{2,1,0:T(8,128)(2,1)}, bf16[2,704,1024]{2,1,0:T(8,128)(2,1)}, f32[2,256,2816]{2,1,0:T(8,128...) custom-call(bf16[66,64,1024]{2,1,0:T(8,128)(2,1)} %summed.1.refs_0_., ...), custom_call_target="tpu_custom_call" | custom-call | flops 86507520 | bytes 95158272 | tf_op jit(solution)/shard_map/stepped/pallas_call | solution.py:585
